TPU v7x, 128 devices: a whole 4x4x4 slice. The times are simulated.
128 devices in a mesh: trade: 8 (over y, core), scen: 16 (over z, x).
Axes of the slice: x: 4, y: 4, z: 4, core: 2. Of those that a mesh axis runs over, the one named last changes fastest.
Arguments:
- factors: float32 [4096, 64], P('scen'), may hold values from -1 to 1
- feat_factor: int32 [1024], replicated, may hold values from 0 to 63
- feat_degree: int32 [1024], replicated, may hold values from 1 to 12
- coefficients: float32 [1024, 16384], P(None, 'trade'), may hold values from -0.1875 to 0.1875
- set_of_trade: int32 [16384], P('trade'), may hold values from 0 to 1023, as said below
- party_of_set: int32 [1024], P('trade'), may hold values from 0 to 1023
- threshold: float32 [1024], replicated, may hold values from 0 to 4
- weight: float32 [1024], replicated, may hold values from 0.5 to 2
Outputs:
- xva: float32 [1024], P('trade')
- coef_sens: float32 [1024, 16384], P('scen', 'trade')
- feature_sens: float32 [1024, 4096], P('trade', 'scen')
Inputs may be any that keep to these rules, and one draw needn't show every extreme that they name: `set_of_trade`: each netting set holds exactly 16 trades; the trades of aligned block b of 2048 trades belong to sets b * 128 to (b + 1) * 128 - 1.
All inputs are finite; a program needn't handle non-finite values.
Results may differ from a plain program's by a relative error of at most 0.000073.
Values sent between devices are 32-bit elements; how exact they have to be, the bound alone decides.
A program may use at most 64 MiB of HBM per device.

v0:
```python
import jax
import jax.numpy as jnp
from jax import lax
from jax.sharding import Mesh
from jax.sharding import PartitionSpec as P

MAXDEG = 12
SET_SIZE = 16
SCEN = ("scen_0", "scen_1")


highest = lax.Precision.HIGHEST


def in_blocks(array, dim, count):
    shape = array.shape
    tiles = array.reshape(*shape[:dim], count, shape[dim] // count, *shape[dim + 1 :])
    return jnp.moveaxis(tiles, dim, 0)


def summed_on_arrival(array, axis, dim):
    count = lax.axis_size(axis)
    tiles = lax.all_to_all(in_blocks(array, dim, count), axis, 0, 0, tiled=True)
    return jnp.sum(tiles, axis=0)


def joined_along(tiles, dim):
    shape = list(tiles.shape[1:])
    shape[dim] *= tiles.shape[0]
    return jnp.moveaxis(tiles, 0, dim).reshape(shape)


def copy_for_each(array, axis):
    count = lax.axis_size(axis)
    return lax.all_to_all(
        jnp.broadcast_to(array[None], (count, *array.shape)), axis, 0, 0, tiled=True
    )


def gather_directly(array, axis, dim):
    return joined_along(copy_for_each(array, axis), dim)


def by_axis(array, axes):
    for axis in axes:
        array = lax.psum(array, axis)
    return array


def chebyshev(points, degrees):
    before = jnp.ones_like(points)
    current = points
    result = jnp.where(degrees[None, :] == 1, current, jnp.zeros_like(points))
    for order in range(2, MAXDEG + 1):
        before, current = (current, 2.0 * points * current - before)
        result = jnp.where(degrees[None, :] == order, current, result)
    return result


def contract(left, right, left_dim, right_dim):
    return lax.dot_general(left, right, (((left_dim,), (right_dim,)), ((), ())), precision=highest)


def local(
    factors, feat_factor, feat_degree, coefficients, set_of_trade, party_of_set, threshold, weight
):
    scen_rows = factors.shape[0]
    scen_total = scen_rows * lax.axis_size(SCEN)
    width = coefficients.shape[0]
    trade_cols = coefficients.shape[1]
    set_count = trade_cols // SET_SIZE
    party_total = threshold.shape[0]
    party_own = party_total // lax.axis_size("trade")
    lookup = (
        lax.broadcasted_iota(jnp.int32, (factors.shape[1], width), 0) == feat_factor[None, :]
    ).astype(jnp.float32)
    points = jnp.dot(factors, lookup, precision=highest)
    phi = chebyshev(points, feat_degree)
    member = (
        set_of_trade[:, None] % set_count
        == lax.broadcasted_iota(jnp.int32, (trade_cols, set_count), 1)
    ).astype(jnp.float32)
    assign = (
        party_of_set[:, None] == lax.broadcasted_iota(jnp.int32, (set_count, party_total), 1)
    ).astype(jnp.float32)
    folded = jnp.dot(coefficients, member, precision=highest)
    exposure = jnp.dot(phi, folded, precision=highest)
    partial_value = jnp.dot(exposure, assign, precision=highest)
    first = lax.axis_index("trade") * party_own
    own_weight = lax.dynamic_slice_in_dim(weight, first, party_own, 0)
    own_sum = summed_on_arrival(partial_value, "trade", 1)
    own_shift = own_sum - lax.dynamic_slice_in_dim(threshold, first, party_own, 0)[None, :]
    own_adj = own_weight[None, :] * jax.nn.sigmoid(own_shift)
    party_adj = gather_directly(own_adj, "trade", 1)
    local_total = own_weight * jnp.sum(jax.nn.softplus(own_shift), axis=0)
    xva = by_axis(local_total, SCEN) / scen_total
    set_adj = contract(party_adj, assign, 1, 1)
    block = phi
    set_grad = summed_on_arrival(contract(block, set_adj, 0, 0) / scen_total, SCEN, 0)
    coef_sens = contract(set_grad, member, 1, 1)
    block = folded
    feature_sens = summed_on_arrival(contract(block, set_adj, 1, 1), "trade", 0)
    return (xva, coef_sens, feature_sens)


def solution(mesh):
    split = Mesh(mesh.devices.reshape(mesh.shape["trade"], 4, 4), ("trade", "scen_0", "scen_1"))
    placed = (P(SCEN, None), P(), P(), P(None, "trade"), P("trade"), P("trade"), P(), P())
    return jax.shard_map(
        local,
        mesh=split,
        in_specs=placed,
        out_specs=(P("trade"), P(SCEN, "trade"), P("trade", SCEN)),
        check_vma=False,
    )
```

profile of v0, /device:TPU:0, one launch (start us, length us, event | category | flops | bytes accessed | tf_op | source)
XLA Modules:
  0.0 103.4 jit_solution(3409343629748093673)
XLA Ops:
  0.7 0.7 broadcast_compare_fusion.11
  1.4 0.7 add_select_fusion
  2.1 8.0 %fusion.9 = f32[128,1024]{1,0:T(8,128)S(1)} fusion(f32[1024,2048]{1,0:T(8,128)} %param.11, s32[2048]{0:T(1024)S(1)} %add_select_fusion), kind=kOutput, calls=%fused_computation.24 | convolution fusion | flops 3221749760 | bytes 8921088 | tf_op jit(solution)/shard_map/dot_general | solution.py:86
  10.2 3.9 %select_select_fusion = f32[256,1024]{0,1:T(8,128)S(1)} fusion(f32[256,64]{0,1:T(8,128)S(1)} %copy-done, pred[1024]{0:T(1024)(128)(4,1)S(1)} %get-tuple-element.15, pred[1024]{0:T(1024)(128)(4,1)S(1)} %get-tuple-element.16, pred[1024]{0:T(1024)(128)(4,1)S(1)} %get-tuple-element.6, pred[1024]{0:T(1024)(128)(4,1)S(1)} %get-tuple-element.7, ...), kind=kOutput, calls=%fused_computation.7 | convolution fusion | flops 210567168 | bytes 1130496 | tf_op jit(solution)/shard_map/dot_general | solution.py:77
  14.1 1.8 %fusion.20 = f32[256,128]{1,0:T(8,128)S(1)} fusion(f32[256,1024]{0,1:T(8,128)S(1)} %select_select_fusion, f32[128,1024]{1,0:T(8,128)S(1)} %fusion.9), kind=kOutput, calls=%fused_computation.54 | convolution fusion | flops 402653184 | bytes 1703936 | tf_op jit(solution)/shard_map/dot_general | solution.py:87
  15.9 0.7 convolution_bitcast_fusion
  16.6 1.1 %copy.17 = f32[32,8,8,128]{3,2,0,1:T(8,128)} copy(f32[32,8,8,128]{3,2,1,0:T(8,128)S(1)} %convolution_bitcast_fusion) | data formatting | bytes 2097152 | tf_op jit(solution)/shard_map/reshape | solution.py:17
  17.7 4.6 %all-to-all-start = ((f32[8,256,128]{2,1,0:T(8,128)}), f32[8,256,128]{2,1,0:T(8,128)S(1)}, u32[]{:S(2)}, u32[]{:S(2)}) async-start(f32[8,256,128]{2,1,0:T(8,128)} %bitcast.27), calls=%async_computation | async-start | bytes 2097152 | tf_op jit(solution)/shard_map/all_to_all | solution.py:23
  22.3 0.8 dynamic_slice.7
  23.0 15.2 %all-to-all-done = f32[8,256,128]{2,1,0:T(8,128)S(1)} async-done(((f32[8,256,128]{2,1,0:T(8,128)}), f32[8,256,128]{2,1,0:T(8,128)S(1)}, u32[]{:S(2)}, u32[]{:S(2)}) %all-to-all-start) | async-done | bytes 1048608 | tf_op jit(solution)/shard_map/all_to_all | solution.py:23
  38.3 0.1 fusion.16
  38.4 0.8 fusion.19
  39.4 18.4 %all_to_all.20 = f32[8,256,128]{1,2,0:T(8,128)S(1)} all-to-all(f32[8,256,128]{1,2,0:T(8,128)S(1)} %broadcast_in_dim.103), channel_id=1, replica_groups=mesh['trade'=8,'scen_0'=4,'scen_1'=4] {'trade'}, dimensions={0} | all-to-all | bytes 2097152 | tf_op jit(solution)/shard_map/all_to_all | solution.py:35
  57.8 1.0 %fusion.11 = f32[256,128]{1,0:T(8,128)S(1)} fusion(f32[256,1024]{0,1:T(8,128)S(1)} %bitcast.28, s32[128]{0:T(128)S(1)} %copy-done.1), kind=kOutput, calls=%fused_computation.26 | convolution fusion | flops 402784256 | bytes 1180160 | tf_op jit(solution)/shard_map/dot_general | solution.py:61
  58.8 1.8 %convolution_multiply_fusion = f32[1024,128]{1,0:T(8,128)} fusion(f32[256,1024]{0,1:T(8,128)S(1)} %select_select_fusion, f32[256,128]{1,0:T(8,128)S(1)} %fusion.11), kind=kOutput, calls=%fused_computation.2 | convolution fusion | flops 402784256 | bytes 1703936 | tf_op jit(solution)/shard_map/dot_general | solution.py:61
  60.6 7.9 %all-to-all-start.2 = ((f32[16,64,128]{2,1,0:T(8,128)}), f32[16,64,128]{2,1,0:T(8,128)S(1)}, u32[]{:S(2)}, u32[]{:S(2)}) async-start(f32[16,64,128]{2,1,0:T(8,128)} %bitcast.4), calls=%async_computation.2 | async-start | bytes 1048576 | tf_op jit(solution)/shard_map/all_to_all | solution.py:23
  68.5 2.0 %fusion.21 = f32[1024,256]{1,0:T(8,128)} fusion(f32[128,1024]{1,0:T(8,128)S(1)} %fusion.9, f32[256,128]{1,0:T(8,128)S(1)} %fusion.11), kind=kOutput, calls=%fused_computation.55 | convolution fusion | flops 402653184 | bytes 1703936 | tf_op jit(solution)/shard_map/dot_general | solution.py:61
  70.5 9.2 %all-to-all-done.2 = f32[16,64,128]{2,1,0:T(8,128)S(1)} async-done(((f32[16,64,128]{2,1,0:T(8,128)}), f32[16,64,128]{2,1,0:T(8,128)S(1)}, u32[]{:S(2)}, u32[]{:S(2)}) %all-to-all-start.2) | async-done | bytes 524320 | tf_op jit(solution)/shard_map/all_to_all | solution.py:23
  79.7 3.6 %all-to-all-start.3 = ((f32[8,128,256]{2,1,0:T(8,128)}), f32[8,128,256]{2,1,0:T(8,128)S(1)}, u32[]{:S(2)}, u32[]{:S(2)}) async-start(f32[8,128,256]{2,1,0:T(8,128)} %bitcast.5), calls=%async_computation.3 | async-start | bytes 2097152 | tf_op jit(solution)/shard_map/all_to_all | solution.py:23
  83.2 8.6 %psum.14 = f32[128]{0:T(128)S(1)} all-reduce(f32[128]{0:T(128)S(1)} %get-tuple-element.3), channel_id=1, replica_groups=mesh['trade'=8,'scen_0'=4,'scen_1'=4] {'scen_0'}, use_global_device_ids=true, to_apply=%region_2.3 | all-reduce | flops 128 | bytes 1024 | tf_op jit(solution)/shard_map/psum | solution.py:46
  91.8 8.6 %psum.15 = f32[128]{0:T(128)S(1)} all-reduce(f32[128]{0:T(128)S(1)} %psum.14), channel_id=1, replica_groups=mesh['trade'=8,'scen_0'=4,'scen_1'=4] {'scen_1'}, use_global_device_ids=true, to_apply=%region_3.4 | all-reduce | flops 128 | bytes 1024 | tf_op jit(solution)/shard_map/psum | solution.py:46
  100.4 0.5 broadcast_multiply_fusion
  101.0 1.7 %fusion = f32[64,2048]{1,0:T(8,128)} fusion(f32[64,128]{1,0:T(8,128)S(1)} %reduce_sum.38, s32[2048]{0:T(1024)S(1)} %add_select_fusion), kind=kOutput, calls=%fused_computation.5 | convolution fusion | flops 201588736 | bytes 565248 | tf_op jit(solution)/shard_map/dot_general | solution.py:61
  102.6 0.7 reduce_sum.39
  (12 shorter events, 0.3 us)
Async XLA Ops:
  0.6 9.5 %copy-start = (f32[256,64]{0,1:T(8,128)S(1)}, f32[256,64]{0,1:T(8,128)}, u32[]{:S(2)}) copy-start(f32[256,64]{0,1:T(8,128)} %param.8) | copy-start | bytes 196612
  0.6 9.5 %copy-start.2 = (s32[1024]{0:T(1024)S(1)}, s32[1024]{0:T(1024)}, u32[]{:S(2)}) copy-start(s32[1024]{0:T(1024)} %param.9) | copy-start | bytes 12292
  10.1 5.8 %copy-start.1 = (s32[128]{0:T(128)S(1)}, s32[128]{0:T(128)}, u32[]{:S(2)}) copy-start(s32[128]{0:T(128)} %param.13) | copy-start | bytes 1540
  17.7 20.5 %all-to-all-start = ((f32[8,256,128]{2,1,0:T(8,128)}), f32[8,256,128]{2,1,0:T(8,128)S(1)}, u32[]{:S(2)}, u32[]{:S(2)}) async-start(f32[8,256,128]{2,1,0:T(8,128)} %bitcast.27), calls=%async_computation | async-start | bytes 2097152 | tf_op jit(solution)/shard_map/all_to_all | solution.py:23
  60.6 19.1 %all-to-all-start.2 = ((f32[16,64,128]{2,1,0:T(8,128)}), f32[16,64,128]{2,1,0:T(8,128)S(1)}, u32[]{:S(2)}, u32[]{:S(2)}) async-start(f32[16,64,128]{2,1,0:T(8,128)} %bitcast.4), calls=%async_computation.2 | async-start | bytes 1048576 | tf_op jit(solution)/shard_map/all_to_all | solution.py:23
  79.7 23.0 %all-to-all-start.3 = ((f32[8,128,256]{2,1,0:T(8,128)}), f32[8,128,256]{2,1,0:T(8,128)S(1)}, u32[]{:S(2)}, u32[]{:S(2)}) async-start(f32[8,128,256]{2,1,0:T(8,128)} %bitcast.5), calls=%async_computation.3 | async-start | bytes 2097152 | tf_op jit(solution)/shard_map/all_to_all | solution.py:23
where the time goes:
time: 104 us; the launch traced here: 103 us
  blocking collectives  35.6 us (34%)
  waiting for transfers between devices  24.3 us (23%)
  matrix products  21 us (20%)
  starting transfers between devices  16 us (15%)
  other arithmetic  3.68 us (4%)
  local copies, waits for them, and re-layouts  2.02 us (2%)
    all_to_all x3, waiting for transfers between devices, summed_on_arrival(): tiles = lax.all_to_all(in_blocks(array, dim, count), axis, 0, 0, tiled=True)  24.3 us
    all_to_all x1, blocking collectives, copy_for_each(): lax.all_to_all(jnp.broadcast_to(array[None], (count, *array.shape)), axis...  18.4 us
    psum x2, blocking collectives, by_axis(): array = lax.psum(array, axis)  17.2 us
    all_to_all x3, starting transfers between devices, summed_on_arrival(): tiles = lax.all_to_all(in_blocks(array, dim, count), axis, 0, 0, tiled=True)  16 us
    dot_general x1, matrix products, local(): folded = jnp.dot(coefficients, member, precision=highest)  8.05 us
    dot_general x4, matrix products, contract(): lax.dot_general(left, right, (((left_dim,), (right_dim,)), ((), ())), pre...  6.51 us
    dot_general x1, matrix products, local(): points = jnp.dot(factors, lookup, precision=highest)  3.94 us
  transfers between devices with their start and end apart: 3, of which 2 were waited for; matrix products, arithmetic and copies ran while one was open for 5% of the time, Pallas kernels for 0%

commit v1 on v0

v1 whole, which is shorter than its diff:
```python
import jax
import jax.numpy as jnp
from jax import lax
from jax.experimental import pallas as pl
from jax.experimental.pallas import tpu as pltpu
from jax.sharding import PartitionSpec as P

MAXDEG = 12
SCEN = 4096
MESH = pl.DeviceIdType.MESH
BF = jnp.bfloat16
F32 = jnp.float32


def mm(left, right):
    return lax.dot_general(left, right, (((1,), (0,)), ((), ())), preferred_element_type=F32)


def mm_nt(left, right):
    return lax.dot_general(left, right, (((1,), (1,)), ((), ())), preferred_element_type=F32)


def halves(value):
    high = value.astype(BF)
    return high, (value - high.astype(F32)).astype(BF)


def thirds(value):
    high = value.astype(BF)
    rest = value - high.astype(F32)
    mid = rest.astype(BF)
    return high, mid, (rest - mid.astype(F32)).astype(BF)


def iota(shape, dim):
    return lax.broadcasted_iota(jnp.int32, shape, dim)


def onehot(mask):
    return jnp.where(mask, 1.0, 0.0).astype(BF)


def upright(row):
    return jnp.broadcast_to(row, (128, 128)).T


def chebyshev_split(points, degrees):
    before = jnp.ones_like(points)
    current = points
    result = jnp.where(degrees == 1, points, 0.0)
    twice = points + points
    for order in range(2, MAXDEG + 1):
        before, current = current, twice * current - before
        result = jnp.where(degrees == order, current, result)
    return halves(result)


def kernel(
    coef_hbm, fac_ref, ff_ref, fd_ref, sot_ref, pos_ref, thr_ref, w_ref,
    xva_out, coef_out, feat_out,
    cbuf, member, memt, pts, phi_h, phi_l, fax, faz, pha_h, pha_l, phb_h, phb_l,
    folded, frows, etb, eh, ehl, party, pcol, same, ownp, tw, sas, sa, sb, sat,
    xs, xr, xt, xz, ga, gb, gra, grb, cst, fst, xst,
    c_sem, p_snd, p_rcv, fx_snd, fx_rcv, fz_snd, fz_rcv, e_snd, e_rcv, f_snd, f_rcv,
    sa_snd, sa_rcv, sb_snd, sb_rcv, st_snd, st_rcv, x_snd, x_rcv, x2_snd, x2_rcv,
    ga_snd, ga_rcv, gb_snd, gb_rcv, o_sem,
):
    t = lax.axis_index("trade")
    sigma = lax.axis_index("scen")
    y, c = t // 2, t % 2
    z, x = sigma // 4, sigma % 4

    def remote(src, dst, snd, rcv, trade, scen):
        return pltpu.make_async_remote_copy(
            src_ref=src, dst_ref=dst, send_sem=snd, recv_sem=rcv,
            device_id=(trade, scen), device_id_type=MESH,
        )

    def tr(k):
        return lax.rem(t + k, 8)

    def xpeer(k):
        return z * 4 + lax.rem(x + k, 4)

    def zpeer(k):
        return lax.rem(z + k, 4) * 4 + x

    loads = []
    for i in range(8):
        rows = pl.ds(128 * i, 128)
        load = pltpu.make_async_copy(coef_hbm.at[rows], cbuf.at[rows], c_sem.at[i])
        load.start()
        loads.append(load)

    barrier = pltpu.get_barrier_semaphore()
    for k in range(1, 8):
        pl.semaphore_signal(barrier, inc=1, device_id=(tr(k), sigma), device_id_type=MESH)
    for k in range(1, 4):
        for d in range(2):
            pl.semaphore_signal(barrier, inc=1, device_id=(2 * y + d, xpeer(k)), device_id_type=MESH)
            pl.semaphore_signal(barrier, inc=1, device_id=(2 * y + d, zpeer(k)), device_id_type=MESH)

    packed = jnp.concatenate([fac_ref[0:128, :], fac_ref[128:256, :]], axis=1)
    fax[x] = packed
    faz[z] = packed

    base = (128 * t).astype(F32)
    lanes = iota((128, 128), 1).astype(F32)
    for j in range(16):
        col = upright(sot_ref[:, 128 * j:128 * j + 128].astype(F32) - base)
        member[128 * j:128 * j + 128, :] = onehot(col == lanes)

    def lookup3(ff, cols, half):
        one = onehot(iota((128, cols), 0) == ff + 64 * half)
        return jnp.concatenate([one, one, one], axis=0)

    three = jnp.concatenate(thirds(packed), axis=1)
    for half in range(2):
        pts[128 * half:128 * half + 128, :] = mm(three, lookup3(ff_ref[...], 1024, half))

    def cheb_own(i, carry):
        cols = pl.ds(pl.multiple_of((i // 4) * 128, 128), 128)
        rows = pl.ds(pl.multiple_of((i % 4) * 64, 64), 64)
        high, low = chebyshev_split(pts[rows, cols], fd_ref[:, cols])
        phi_h[rows, cols] = high
        phi_l[rows, cols] = low
        return carry

    lax.fori_loop(0, 32, cheb_own, 0)

    pl.semaphore_wait(barrier, 19)

    party_sends = []
    for k in range(1, 8):
        send = remote(pos_ref, party.at[t], p_snd.at[k - 1], p_rcv.at[t], tr(k), sigma)
        send.start()
        party_sends.append(send)
    fac_sends = []
    for k in range(1, 4):
        send = remote(fax.at[x], fax.at[x], fx_snd.at[k - 1], fx_rcv.at[x], t, xpeer(k))
        send.start()
        fac_sends.append(send)
        send = remote(faz.at[z], faz.at[z], fz_snd.at[k - 1], fz_rcv.at[z], t, zpeer(k))
        send.start()
        fac_sends.append(send)
    party[t] = pos_ref[...]

    for i in range(8):
        loads[i].wait()
        rows = slice(128 * i, 128 * i + 128)
        high, low = halves(cbuf[rows, :])
        folded[i] = mm(high, member[...]) + mm(low, member[...])
    exposure = jnp.zeros((256, 128), F32)
    for i in range(8):
        cols = slice(128 * i, 128 * i + 128)
        high, low = halves(folded[i])
        wide = mm(phi_h[:, cols], jnp.concatenate([high, low], axis=1))
        exposure = exposure + wide[:, :128] + wide[:, 128:] + mm(phi_l[:, cols], high)
    etb[0] = exposure[0:128, :].T
    etb[1] = exposure[128:256, :].T

    e_sends = []
    for k in (4, 5, 3, 2, 6, 7, 1):
        other = tr(k)
        send = remote(etb.at[other % 2], eh.at[t], e_snd.at[k - 1], e_rcv.at[t], other, sigma)
        send.start()
        e_sends.append(send)
    f_sends = []
    for k in (4, 5, 3, 2, 6, 7, 1):
        other = tr(k)
        send = remote(folded.at[other], frows.at[t], f_snd.at[k - 1], f_rcv.at[t], other, sigma)
        send.start()
        f_sends.append(send)
    eh[t] = etb[c]
    frows[t] = folded[t]

    for k in range(1, 8):
        src = tr(k)
        remote(pos_ref, party.at[src], p_snd.at[k - 1], p_rcv.at[src], src, sigma).wait_recv()
    for j in range(8):
        pcol[j] = upright(party[j].astype(F32))
    table = thirds(thr_ref[...]) + thirds(w_ref[...])
    table = jnp.concatenate([part.astype(F32) for part in table] + [jnp.zeros((2, 1024), F32)], axis=0).astype(BF)

    def rows_of(j, carry):
        col = pcol[j]
        rows = pl.ds(pl.multiple_of(j * 128, 128), 128)
        for i in range(8):
            same[rows, 128 * i:128 * i + 128] = onehot(col == party[i].astype(F32))
        spread = jnp.concatenate([onehot(col == lanes + 128.0 * i) for i in range(8)], axis=1)
        tw[j] = mm_nt(spread, table)
        return carry

    lax.fori_loop(0, 8, rows_of, 0)
    for i in range(8):
        ownp[:, 128 * i:128 * i + 128] = onehot(iota((256, 128), 0) + 256 * y == party[i])

    fvals = jnp.concatenate([ff_ref[...].astype(F32), fd_ref[...].astype(F32), jnp.zeros((6, 1024), F32)], axis=0).astype(BF)
    lane256 = iota((1024, 256), 1)
    fidx_a = ((lane256 // 64) * 4 + x) * 64 + lane256 % 64
    fidx_b = z * 256 + lane256
    picks = []
    for fidx in (fidx_a, fidx_b):
        picked = mm(fvals, onehot(iota((1024, 256), 0) == fidx)).astype(jnp.int32)
        picks.append((picked[0:1, :], picked[1:2, :]))

    def phi_of(buf, ff, fd, out_h, out_l):
        for half in range(2):
            look = lookup3(ff, 256, half)
            for q in range(4):
                pts[0:128, 256 * q:256 * q + 256] = mm(jnp.concatenate(thirds(buf[q]), axis=1), look)
            for q in range(4):
                for b in range(2):
                    def cheb(r, carry, q=q, b=b):
                        rows = pl.ds(pl.multiple_of(r * 64, 64), 64)
                        high, low = chebyshev_split(
                            pts[rows, 256 * q + 128 * b:256 * q + 128 * b + 128], fd[:, 128 * b:128 * b + 128]
                        )
                        out_h[2 * q + half, rows, 128 * b:128 * b + 128] = high
                        out_l[2 * q + half, rows, 128 * b:128 * b + 128] = low
                        return carry

                    lax.fori_loop(0, 2, cheb, 0)

    for k in range(1, 4):
        src = lax.rem(x + k, 4)
        remote(fax.at[x], fax.at[src], fx_snd.at[k - 1], fx_rcv.at[src], t, xpeer(k)).wait_recv()
    phi_of(fax, picks[0][0], picks[0][1], pha_h, pha_l)
    for k in range(1, 4):
        src = lax.rem(z + k, 4)
        remote(faz.at[z], faz.at[src], fz_snd.at[k - 1], fz_rcv.at[src], t, zpeer(k)).wait_recv()
    phi_of(faz, picks[1][0], picks[1][1], phb_h, phb_l)

    for k in range(1, 8):
        src = tr(k)
        remote(etb.at[0], eh.at[src], e_snd.at[k - 1], e_rcv.at[src], src, sigma).wait_recv()
    for j in range(8):
        high, low = halves(eh[j])
        ehl[128 * j:128 * j + 128, 0:128] = high
        ehl[128 * j:128 * j + 128, 128:256] = low

    def adjoint(j):
        rows = pl.ds(pl.multiple_of(j * 128, 128), 128)
        wide = mm(same[rows, :], ehl[...])
        consts = tw[j]
        shift = consts[:, 0:1] + consts[:, 1:2] + consts[:, 2:3]
        scale = consts[:, 3:4] + consts[:, 4:5] + consts[:, 5:6]
        return scale * jax.nn.sigmoid(wide[:, :128] + wide[:, 128:] - shift)

    for d in range(2):
        sas[d] = adjoint(2 * y + d)
    s_sends = []
    for k in range(0, 4):
        for e in range(2):
            if k == 0 and e == 0:
                continue
            d = lax.rem(c + e, 2)
            i = 2 * k + e - 1
            send = remote(sas.at[d, pl.ds(0, 64)], sa.at[2 * x + c], sa_snd.at[i], sa_rcv.at[2 * x + c], 2 * y + d, xpeer(k))
            send.start()
            s_sends.append(send)
            send = remote(sas.at[d, pl.ds(64, 64)], sb.at[2 * z + c], sb_snd.at[i], sb_rcv.at[2 * z + c], 2 * y + d, zpeer(k))
            send.start()
            s_sends.append(send)
    sa[2 * x + c] = sas[c, 0:64, :]
    sb[2 * z + c] = sas[c, 64:128, :]

    def other_rows(j, carry):
        sat[c, j] = adjoint(j)
        return carry

    lax.fori_loop(0, 8, other_rows, 0)
    partner = 2 * y + 1 - c
    sat_send = remote(sat.at[c], sat.at[c], st_snd, st_rcv, partner, sigma)
    sat_send.start()

    wide = mm(ownp[...], ehl[...])
    for d in range(2):
        first = pl.multiple_of(256 * y + 128 * d, 128)
        limit = upright(thr_ref[:, pl.ds(first, 128)])
        soft = jax.nn.softplus(wide[128 * d:128 * d + 128, :128] + wide[128 * d:128 * d + 128, 128:] - limit)
        xs[d] = jnp.broadcast_to(jnp.sum(soft.T, axis=0, keepdims=True), (8, 128))
    x_sends = []
    for k in range(0, 4):
        for e in range(2):
            if k == 0 and e == 0:
                continue
            d = lax.rem(c + e, 2)
            send = remote(xs.at[d], xr.at[2 * x + c], x_snd.at[2 * k + e - 1], x_rcv.at[2 * x + c], 2 * y + d, xpeer(k))
            send.start()
            x_sends.append(send)
    xr[2 * x + c] = xs[c]

    for k in range(1, 8):
        src = tr(k)
        remote(folded.at[0], frows.at[src], f_snd.at[k - 1], f_rcv.at[src], src, sigma).wait_recv()
    remote(sat.at[c], sat.at[1 - c], st_snd, st_rcv, partner, sigma).wait_recv()
    sums = [jnp.zeros((128, 128), F32) for _ in range(2)]
    for j in range(8):
        left_h, left_l = halves(frows[j])
        for d in range(2):
            high, low = halves(sat[d, j])
            sums[d] = sums[d] + mm(left_h, high) + mm(left_h, low) + mm(left_l, high)
    fst[:, 0:128] = sums[0]
    fst[:, 128:256] = sums[1]
    feat_copy = pltpu.make_async_copy(fst, feat_out, o_sem.at[0])
    feat_copy.start()

    low_lanes = iota((32, 128), 1) < 64

    def gradient(slots, out_h, out_l, dest):
        total = jnp.zeros((64, 256), F32)
        for j in range(8):
            high, low = halves(slots[j])
            total = total + mm(high, out_h[j]) + mm(low, out_h[j]) + mm(high, out_l[j])
        for pair in range(2):
            top = total[0:32, 128 * pair:128 * pair + 128]
            bottom = total[32:64, 128 * pair:128 * pair + 128]
            dest[2 * pair] = jnp.where(low_lanes, top, pltpu.roll(bottom, 64, 1))
            dest[2 * pair + 1] = jnp.where(low_lanes, pltpu.roll(top, 64, 1), bottom)

    def wait_slots(buf, rcv, snd, mine, peer):
        for k in range(0, 4):
            for e in range(2):
                if k == 0 and e == 0:
                    continue
                d = lax.rem(c + e, 2)
                slot = 2 * lax.rem(mine + k, 4) + d
                remote(buf.at[slot], buf.at[slot], snd.at[2 * k + e - 1], rcv.at[slot], 2 * y + d, peer(k)).wait_recv()

    g_sends = []
    wait_slots(sa, sa_rcv, sa_snd, x, xpeer)
    gradient(sa, pha_h, pha_l, ga)
    for k in (2, 1, 3):
        send = remote(ga.at[lax.rem(z + k, 4)], gra.at[z], ga_snd.at[k - 1], ga_rcv.at[z], t, zpeer(k))
        send.start()
        g_sends.append(send)
    wait_slots(sb, sb_rcv, sb_snd, z, zpeer)
    gradient(sb, phb_h, phb_l, gb)
    for k in (2, 1, 3):
        send = remote(gb.at[lax.rem(x + k, 4)], grb.at[x], gb_snd.at[k - 1], gb_rcv.at[x], t, xpeer(k))
        send.start()
        g_sends.append(send)
    gra[z] = ga[z]
    grb[x] = gb[x]

    wait_slots(xr, x_rcv, x_snd, x, xpeer)
    part = xr[0]
    for j in range(1, 8):
        part = part + xr[j]
    xt[...] = part
    for k in range(1, 4):
        send = remote(xt, xz.at[z], x2_snd.at[k - 1], x2_rcv.at[z], t, zpeer(k))
        send.start()
        x_sends.append(send)
    xz[z] = part

    row = iota((128, 128), 0)
    of_row = (row // 64) * 32 + ((row % 64) // 32) * 64 + row % 32 + 128 * t
    for j in range(16):
        memt[:, 128 * j:128 * j + 128] = onehot(of_row == sot_ref[:, 128 * j:128 * j + 128])

    for k in range(1, 4):
        src = lax.rem(z + k, 4)
        remote(ga.at[0], gra.at[src], ga_snd.at[k - 1], ga_rcv.at[src], t, zpeer(k)).wait_recv()
    for k in range(1, 4):
        src = lax.rem(x + k, 4)
        remote(gb.at[0], grb.at[src], gb_snd.at[k - 1], gb_rcv.at[src], t, xpeer(k)).wait_recv()
    grad_a = (gra[0] + gra[1]) + (gra[2] + gra[3])
    grad_b = (grb[0] + grb[1]) + (grb[2] + grb[3])
    grads = (jnp.concatenate([grad_a, grad_b], axis=0) * (1.0 / SCEN)).T
    high, low = halves(grads)
    even, odd = memt[0:64, :], memt[64:128, :]
    cst[...] = (mm(high[0:64], even) + mm(low[0:64], even)) + (mm(high[64:128], odd) + mm(low[64:128], odd))
    coef_copy = pltpu.make_async_copy(cst, coef_out, o_sem.at[1])
    coef_copy.start()

    for k in range(1, 4):
        src = lax.rem(z + k, 4)
        remote(xt, xz.at[src], x2_snd.at[k - 1], x2_rcv.at[src], t, zpeer(k)).wait_recv()
    whole = (xz[0] + xz[1]) + (xz[2] + xz[3])
    first = pl.multiple_of(128 * t, 128)
    xst[...] = w_ref[:, pl.ds(first, 128)] * whole[0:1, :] * (1.0 / SCEN)
    xva_copy = pltpu.make_async_copy(xst, xva_out, o_sem.at[2])
    xva_copy.start()

    for send in party_sends + fac_sends + e_sends + f_sends + s_sends + [sat_send] + x_sends + g_sends:
        send.wait_send()
    feat_copy.wait()
    coef_copy.wait()
    xva_copy.wait()


def local(factors, feat_factor, feat_degree, coefficients, set_of_trade, party_of_set, threshold, weight):
    vmem = pl.BlockSpec(memory_space=pltpu.VMEM)
    anywhere = pl.BlockSpec(memory_space=pl.ANY)
    V = pltpu.VMEM
    D = pltpu.SemaphoreType.DMA
    scratch = [
        V((1024, 2048), F32),
        V((2048, 128), BF),
        V((128, 2048), BF),
        V((256, 1024), F32),
        V((256, 1024), BF), V((256, 1024), BF),
        V((4, 128, 128), F32), V((4, 128, 128), F32),
        V((8, 128, 256), BF), V((8, 128, 256), BF), V((8, 128, 256), BF), V((8, 128, 256), BF),
        V((8, 128, 128), F32),
        V((8, 128, 128), F32),
        V((2, 128, 128), F32),
        V((8, 128, 128), F32),
        V((1024, 256), BF),
        V((8, 1, 128), jnp.int32),
        V((8, 128, 128), F32),
        V((1024, 1024), BF),
        V((256, 1024), BF),
        V((8, 128, 8), F32),
        V((2, 128, 128), F32),
        V((8, 64, 128), F32), V((8, 64, 128), F32),
        V((2, 8, 128, 128), F32),
        V((2, 8, 128), F32), V((8, 8, 128), F32), V((8, 128), F32), V((4, 8, 128), F32),
        V((4, 32, 128), F32), V((4, 32, 128), F32), V((4, 32, 128), F32), V((4, 32, 128), F32),
        V((64, 2048), F32), V((128, 256), F32), V((1, 128), F32),
        D((8,)), D((7,)), D((8,)), D((3,)), D((4,)), D((3,)), D((4,)), D((7,)), D((8,)), D((7,)), D((8,)),
        D((7,)), D((8,)), D((7,)), D((8,)), D(()), D(()), D((7,)), D((8,)), D((3,)), D((4,)),
        D((3,)), D((4,)), D((3,)), D((4,)), D((3,)),
    ]
    xva, coef_sens, feature_sens = pl.pallas_call(
        kernel,
        out_shape=(
            jax.ShapeDtypeStruct((1, 128), F32),
            jax.ShapeDtypeStruct((64, 2048), F32),
            jax.ShapeDtypeStruct((128, 256), F32),
        ),
        in_specs=[anywhere] + [vmem] * 7,
        out_specs=(anywhere, anywhere, anywhere),
        scratch_shapes=scratch,
        compiler_params=pltpu.CompilerParams(collective_id=0, has_side_effects=True, vmem_limit_bytes=48 << 20),
    )(
        coefficients, factors, feat_factor.reshape(1, -1), feat_degree.reshape(1, -1),
        set_of_trade.reshape(1, -1), party_of_set.reshape(1, -1), threshold.reshape(1, -1), weight.reshape(1, -1),
    )
    return xva.reshape(-1), coef_sens, feature_sens


def solution(mesh):
    placed = (P("scen", None), P(), P(), P(None, "trade"), P("trade"), P("trade"), P(), P())
    return jax.shard_map(
        local,
        mesh=mesh,
        in_specs=placed,
        out_specs=(P("trade"), P("scen", "trade"), P("trade", "scen")),
        check_vma=False,
    )
```

time: 104 us -> 40.5 us (0.39)
  blocking collectives: 35.6 us -> 0 us
  Pallas kernels: 0 us -> 32.5 us
  waiting for transfers between devices: 24.3 us -> 0 us
  matrix products: 21 us -> 0 us
  starting transfers between devices: 16 us -> 0 us
  local copies, waits for them, and re-layouts: 2.02 us -> 6.99 us
  other arithmetic: 3.68 us -> 0 us
    pallas_call x0 -> x1, Pallas kernels: none -> 32.5 us  [local(): pl.pallas_call(kernel, out_shape=(jax.ShapeDtypeStruct((1, 128), F32), ja...]
    all_to_all x3 -> x0, waiting for transfers between devices: 24.3 us -> none  [summed_on_arrival(): tiles = lax.all_to_all(in_blocks(array, dim, count), axis, 0, 0, tiled=True)]
    dot_general x8 -> x0, matrix products: 21 us -> none  [the longest x1 8.05 us: local(): folded = jnp.dot(coefficients, member, precision=highest)]
    all_to_all x1 -> x0, blocking collectives: 18.4 us -> none  [copy_for_each(): lax.all_to_all(jnp.broadcast_to(array[None], (count, *array.shape)), axis...]
    psum x2 -> x0, blocking collectives: 17.2 us -> none  [by_axis(): array = lax.psum(array, axis)]
    all_to_all x3 -> x0, starting transfers between devices: 16 us -> none  [summed_on_arrival(): tiles = lax.all_to_all(in_blocks(array, dim, count), axis, 0, 0, tiled=True)]
    unnamed x6 -> x16, local copies, waits for them, and re-layouts: 0.02 us -> 6.99 us
    reshape x1 -> x0, local copies, waits for them, and re-layouts: 1.06 us -> none  [in_blocks(): array.reshape(*shape[:dim], count, shape[dim] // count, *shape[dim + 1:])]
  transfers between devices with their start and end apart: 3 -> 0, of which waited for: 2 -> 0; matrix products, arithmetic and copies ran while one was open for 5% -> 0% of each run, Pallas kernels for 0% -> 0%
where the time goes in v1:
time: 40.5 us; the launch traced here: 40.1 us
  Pallas kernels  32.5 us (80%)
  local copies, waits for them, and re-layouts  6.99 us (17%)
  between operations  0.66 us (2%)
    pallas_call x1, Pallas kernels, local(): pl.pallas_call(kernel, out_shape=(jax.ShapeDtypeStruct((1, 128), F32), ja...  32.5 us
    unnamed x16, local copies, waits for them, and re-layouts  6.99 us

profile of v1, /device:TPU:0, one launch (start us, length us, event | category | flops | bytes accessed | tf_op | source)
XLA Modules:
  0.0 40.1 jit_solution(7245567392550454436)
XLA Ops:
  0.6 0.9 %copy.11.fac_ref = f32[256,64]{1,0:T(8,128)S(1)} copy(f32[256,64]{0,1:T(8,128)} %param.8) | data formatting | bytes 131072 | tf_op args[0]
  1.6 0.0 copy-start
  1.6 0.7 %copy-done = s32[2048]{0:T(1024)S(1)} copy-done((s32[2048]{0:T(1024)S(1)}, s32[2048]{0:T(1024)}, u32[]{:S(2)}) %copy-start) | copy-done | bytes 8216
  2.3 0.0 copy-start.1
  2.3 0.7 %copy-done.1 = s32[1024]{0:T(1024)S(1)} copy-done((s32[1024]{0:T(1024)S(1)}, s32[1024]{0:T(1024)}, u32[]{:S(2)}) %copy-start.1) | copy-done | bytes 4120
  3.0 0.0 copy-start.2
  3.0 0.7 %copy-done.2 = s32[1024]{0:T(1024)S(1)} copy-done((s32[1024]{0:T(1024)S(1)}, s32[1024]{0:T(1024)}, u32[]{:S(2)}) %copy-start.2) | copy-done | bytes 4120
  3.6 0.0 copy-start.3
  3.6 0.7 %copy-done.3 = f32[1024]{0:T(1024)S(1)} copy-done((f32[1024]{0:T(1024)S(1)}, f32[1024]{0:T(1024)}, u32[]{:S(2)}) %copy-start.3) | copy-done | bytes 4120
  4.3 0.0 copy-start.4
  4.3 0.7 %copy-done.4 = f32[1024]{0:T(1024)S(1)} copy-done((f32[1024]{0:T(1024)S(1)}, f32[1024]{0:T(1024)}, u32[]{:S(2)}) %copy-start.4) | copy-done | bytes 4120
  5.0 0.0 copy-start.5
  5.0 0.7 %copy-done.5 = s32[128]{0:T(128)S(1)} copy-done((s32[128]{0:T(128)S(1)}, s32[128]{0:T(128)}, u32[]{:S(2)}) %copy-start.5) | copy-done | bytes 536
  5.7 32.5 %shard_map.103 = (f32[1,128]{1,0:T(1,128)S(1)}, f32[64,2048]{1,0:T(8,128)S(1)}, f32[128,256]{1,0:T(8,128)S(1)}) custom-call(f32[1024,2048]{1,0:T(8,128)} %coef_hbm.1, f32[256,64]{1,0:T(8,128)S(1)} %copy.11.fac_ref, s32[1,1024]{1,0:T(1,128)S(1)} %bitcast.8, s32[1,1024]{1,0:T(1,128)S(1)} %bitcast.9, s32[1,2048]{1,0:T(1,128)S(1)} %bitcast.7, ...), custom_call_target="tpu_custom_call" | custom-call | tf_op jit(solution)/shard_map/pallas_call | solution.py:427
  38.2 0.5 %copy.15 = f32[128]{0:T(128)} copy(f32[128]{0:T(128)S(1)} %bitcast.13) | data formatting | bytes 1024
  38.7 0.8 %copy.16 = f32[64,2048]{1,0:T(8,128)} copy(f32[64,2048]{1,0:T(8,128)S(1)} %get-tuple-element.13) | data formatting | bytes 1048576
  39.5 0.7 %copy.17 = f32[128,256]{1,0:T(8,128)} copy(f32[128,256]{1,0:T(8,128)S(1)} %get-tuple-element.14) | data formatting | bytes 262144
Async XLA Ops:
  1.6 0.7 %copy-start = (s32[2048]{0:T(1024)S(1)}, s32[2048]{0:T(1024)}, u32[]{:S(2)}) copy-start(s32[2048]{0:T(1024)} %param.12) | copy-start | bytes 24580
  2.3 0.7 %copy-start.1 = (s32[1024]{0:T(1024)S(1)}, s32[1024]{0:T(1024)}, u32[]{:S(2)}) copy-start(s32[1024]{0:T(1024)} %param.9) | copy-start | bytes 12292
  3.0 0.7 %copy-start.2 = (s32[1024]{0:T(1024)S(1)}, s32[1024]{0:T(1024)}, u32[]{:S(2)}) copy-start(s32[1024]{0:T(1024)} %param.10) | copy-start | bytes 12292
  3.6 0.7 %copy-start.3 = (f32[1024]{0:T(1024)S(1)}, f32[1024]{0:T(1024)}, u32[]{:S(2)}) copy-start(f32[1024]{0:T(1024)} %param.14) | copy-start | bytes 12292
  4.3 0.7 %copy-start.4 = (f32[1024]{0:T(1024)S(1)}, f32[1024]{0:T(1024)}, u32[]{:S(2)}) copy-start(f32[1024]{0:T(1024)} %param.15) | copy-start | bytes 12292
  5.0 0.7 %copy-start.5 = (s32[128]{0:T(128)S(1)}, s32[128]{0:T(128)}, u32[]{:S(2)}) copy-start(s32[128]{0:T(128)} %param.13) | copy-start | bytes 1540

commit v2 on v1

v2 whole, which is shorter than its diff:
```python
import jax
import jax.numpy as jnp
from jax import lax
from jax.experimental import pallas as pl
from jax.experimental.pallas import tpu as pltpu
from jax.sharding import PartitionSpec as P

MAXDEG = 12
SCEN = 4096
MESH = pl.DeviceIdType.MESH
BF = jnp.bfloat16
F32 = jnp.float32


def mm(left, right):
    return lax.dot_general(left, right, (((1,), (0,)), ((), ())), preferred_element_type=F32)


def mm_nt(left, right):
    return lax.dot_general(left, right, (((1,), (1,)), ((), ())), preferred_element_type=F32)


def halves(value):
    high = value.astype(BF)
    return high, (value - high.astype(F32)).astype(BF)


def thirds(value):
    high = value.astype(BF)
    rest = value - high.astype(F32)
    mid = rest.astype(BF)
    return high, mid, (rest - mid.astype(F32)).astype(BF)


def iota(shape, dim):
    return lax.broadcasted_iota(jnp.int32, shape, dim)


def onehot(mask):
    return jnp.where(mask, 1.0, 0.0).astype(BF)


def upright(row):
    return jnp.broadcast_to(row, (128, 128)).T


def degree_basis(dup, out_h, out_l):
    low = iota((64, 128), 1) < 64
    for r in range(4):
        rows = slice(64 * r, 64 * r + 64)
        current = dup[rows, :]
        twice = current + current
        before = jnp.ones_like(current)
        for pair in range(MAXDEG // 2):
            after = twice * current - before
            cols = slice(128 * pair, 128 * pair + 128)
            out_h[rows, cols], out_l[rows, cols] = halves(jnp.where(low, current, after))
            if pair < MAXDEG // 2 - 1:
                before, current = after, twice * after - current


def kernel(
    coef_hbm, fac_hbm, ff_hbm, fd_hbm, sot_hbm, pos_hbm, thr_hbm, w_hbm,
    xva_out, coef_out, feat_out,
    ff_ref, fd_ref, sot_ref, pos_ref, thr_ref, w_ref, cbuf,
    member, memt, pick, dup, th, tl, fax, faz, pha_h, pha_l, phb_h, phb_l,
    folded, gsum, frows, etb, eh, ehl, party, pcol, same, ownp, tw, sas, sa, sb, sat,
    xs, xr, xt, xz, ga, gb, gra, grb, i_sem,
    c_sem, p_snd, p_rcv, fx_snd, fx_rcv, fz_snd, fz_rcv, e_snd, e_rcv, f_snd, f_rcv,
    sa_snd, sa_rcv, sb_snd, sb_rcv, st_snd, st_rcv, x_snd, x_rcv, x2_snd, x2_rcv,
    ga_snd, ga_rcv, gb_snd, gb_rcv,
):
    t = lax.axis_index("trade")
    sigma = lax.axis_index("scen")
    y, c = t // 2, t % 2
    z, x = sigma // 4, sigma % 4
    partner = 2 * y + 1 - c

    def remote(src, dst, snd, rcv, trade, scen):
        return pltpu.make_async_remote_copy(
            src_ref=src, dst_ref=dst, send_sem=snd, recv_sem=rcv,
            device_id=(trade, scen), device_id_type=MESH,
        )

    def tr(k):
        return lax.rem(t + k, 8)

    def xpeer(k):
        return z * 4 + lax.rem(x + k, 4)

    def zpeer(k):
        return lax.rem(z + k, 4) * 4 + x

    class Gather:
        def __init__(self, slots, snd, rcv, mine, place):
            self.slots, self.snd, self.rcv, self.mine, self.place = slots, snd, rcv, mine, place
            self.sends = []

        def put(self, src, slot, i, k, d):
            trade, scen = self.place(k, d)
            send = remote(src, self.slots.at[slot], self.snd.at[i], self.rcv.at[slot], trade, scen)
            send.start()
            self.sends.append(send)

        def start(self, piece):
            slot = 2 * self.mine + c
            self.put(piece(c), slot, 0, 1, c)
            self.put(piece(1 - c), slot, 1, 3, 1 - c)
            self.put(piece(1 - c), slot, 2, 1, 1 - c)
            self.put(piece(c), slot, 3, 3, c)
            self.put(piece(1 - c), slot, 4, 0, 1 - c)

        def wait_slot(self, k, e):
            slot = 2 * lax.rem(self.mine + k, 4) + lax.rem(c + e, 2)
            trade, scen = self.place(k, lax.rem(c + e, 2)) if k or e else self.place(0, 1 - c)
            remote(self.slots.at[slot], self.slots.at[slot], self.snd.at[0], self.rcv.at[slot], trade, scen).wait_recv()
            return slot

        def forward(self):
            slot = self.wait_slot(3, 0)
            self.put(self.slots.at[slot], slot, 5, 1, c)
            slot = self.wait_slot(1, 1)
            self.put(self.slots.at[slot], slot, 6, 3, c)

        def finish(self):
            for k, e in ((0, 1), (3, 1), (1, 0), (2, 0), (2, 1)):
                self.wait_slot(k, e)

    smalls = []
    for i, (src, dst) in enumerate((
        (sot_hbm, sot_ref), (ff_hbm, ff_ref), (fd_hbm, fd_ref), (fac_hbm, fax.at[x]), (fac_hbm, faz.at[z]),
        (pos_hbm, pos_ref), (thr_hbm, thr_ref), (w_hbm, w_ref),
    )):
        small = pltpu.make_async_copy(src, dst, i_sem.at[i])
        small.start()
        smalls.append(small)
    loads = []
    for i in range(8):
        rows = pl.ds(128 * i, 128)
        load = pltpu.make_async_copy(coef_hbm.at[rows], cbuf.at[rows], c_sem.at[i])
        load.start()
        loads.append(load)

    barrier = pltpu.get_barrier_semaphore()
    for k in range(1, 8):
        pl.semaphore_signal(barrier, inc=1, device_id=(tr(k), sigma), device_id_type=MESH)
    for k in range(1, 4):
        for d in range(2):
            pl.semaphore_signal(barrier, inc=1, device_id=(2 * y + d, xpeer(k)), device_id_type=MESH)
            pl.semaphore_signal(barrier, inc=1, device_id=(2 * y + d, zpeer(k)), device_id_type=MESH)

    for small in smalls:
        small.wait()

    base = (128 * t).astype(F32)
    lanes = iota((128, 128), 1).astype(F32)
    for j in range(16):
        col = upright(sot_ref[:, 128 * j:128 * j + 128].astype(F32) - base)
        member[128 * j:128 * j + 128, :] = onehot(col == lanes)

    def doubled(facts):
        return jnp.concatenate([facts, facts], axis=0).T

    degree_basis(doubled(fax[x]), th, tl)

    keys = (fd_ref[...] - 1) * 64 + ff_ref[...]
    for i in range(4):
        loads[2 * i].wait()
        loads[2 * i + 1].wait()
        rows = slice(256 * i, 256 * i + 256)
        high, low = halves(cbuf[rows, :])
        fold = mm(high, member[...]) + mm(low, member[...])
        folded[2 * i] = fold[:128, :]
        folded[2 * i + 1] = fold[128:, :]
        spot = onehot(iota((768, 256), 0) == keys[:, rows])
        wide = mm(spot, jnp.concatenate(halves(fold), axis=1))
        wide = wide[:, :128] + wide[:, 128:]
        if i == 0:
            gsum[...] = wide
        elif i < 3:
            gsum[...] += wide
        else:
            total = gsum[...] + wide
    high, low = halves(total)
    wide = mm(th[...], jnp.concatenate([high, low], axis=1))
    exposure = wide[:, :128] + wide[:, 128:] + mm(tl[...], high)
    etb[0] = exposure[0:128, :].T
    etb[1] = exposure[128:256, :].T

    pl.semaphore_wait(barrier, 19)

    e_all = Gather(eh, e_snd, e_rcv, y, lambda k, d: (2 * lax.rem(y + k, 4) + d, sigma))
    e_all.start(lambda d: etb.at[d])

    party_sends = []
    for k in range(1, 8):
        send = remote(pos_ref, party.at[t], p_snd.at[k - 1], p_rcv.at[t], tr(k), sigma)
        send.start()
        party_sends.append(send)
    fac_sends = []
    for k in range(1, 4):
        send = remote(fax.at[x], fax.at[x], fx_snd.at[k - 1], fx_rcv.at[x], t, xpeer(k))
        send.start()
        fac_sends.append(send)
        send = remote(faz.at[z], faz.at[z], fz_snd.at[k - 1], fz_rcv.at[z], t, zpeer(k))
        send.start()
        fac_sends.append(send)
    party[t] = pos_ref[...]
    eh[t] = etb[c]
    frows[t] = folded[t]

    fvals = jnp.concatenate([ff_ref[...].astype(F32), fd_ref[...].astype(F32), jnp.zeros((6, 1024), F32)], axis=0).astype(BF)
    lane256 = iota((1024, 256), 1)
    fidx_a = ((lane256 // 64) * 4 + x) * 64 + lane256 % 64
    fidx_b = z * 256 + lane256
    for i, fidx in enumerate((fidx_a, fidx_b)):
        picked = mm(fvals, onehot(iota((1024, 256), 0) == fidx)).astype(jnp.int32)
        pick[i] = onehot(iota((768, 256), 0) == (picked[1:2, :] - 1) * 64 + picked[0:1, :])

    for k in range(1, 8):
        src = tr(k)
        remote(pos_ref, party.at[src], p_snd.at[k - 1], p_rcv.at[src], src, sigma).wait_recv()
    for j in range(8):
        pcol[j] = upright(party[j].astype(F32))
    table = thirds(thr_ref[...]) + thirds(w_ref[...])
    table = jnp.concatenate([part.astype(F32) for part in table] + [jnp.zeros((2, 1024), F32)], axis=0).astype(BF)

    def rows_of(j, carry):
        col = pcol[j]
        rows = pl.ds(pl.multiple_of(j * 128, 128), 128)
        for i in range(8):
            same[rows, 128 * i:128 * i + 128] = onehot(col == party[i].astype(F32))
        spread = jnp.concatenate([onehot(col == lanes + 128.0 * i) for i in range(8)], axis=1)
        tw[j] = mm_nt(spread, table)
        return carry

    lax.fori_loop(0, 8, rows_of, 0)

    e_all.forward()

    def phi_of(buf, which, out_h, out_l):
        def block(q, carry):
            degree_basis(doubled(buf[q]), th, tl)
            out_h[q] = mm(th[...], pick[which]).astype(BF)
            out_l[q] = mm(tl[...], pick[which]).astype(BF)
            return carry

        lax.fori_loop(0, 4, block, 0)

    for k in range(1, 4):
        src = lax.rem(x + k, 4)
        remote(fax.at[x], fax.at[src], fx_snd.at[k - 1], fx_rcv.at[src], t, xpeer(k)).wait_recv()
    phi_of(fax, 0, pha_h, pha_l)

    e_all.finish()
    for j in range(8):
        high, low = halves(eh[j])
        ehl[128 * j:128 * j + 128, 0:128] = high
        ehl[128 * j:128 * j + 128, 128:256] = low

    def adjoint(j, blocks=1):
        rows = pl.ds(pl.multiple_of(j * 128, 128), 128)
        wide = mm(same[rows, :], ehl[...])
        consts = tw[j]
        shift = consts[:, 0:1] + consts[:, 1:2] + consts[:, 2:3]
        scale = consts[:, 3:4] + consts[:, 4:5] + consts[:, 5:6]
        return scale * jax.nn.sigmoid(wide[:, :128] + wide[:, 128:] - shift)

    for d in range(2):
        sas[d] = adjoint(2 * y + d)

    a_all = Gather(sa, sa_snd, sa_rcv, x, lambda k, d: (2 * y + d, xpeer(k)))
    b_all = Gather(sb, sb_snd, sb_rcv, z, lambda k, d: (2 * y + d, zpeer(k)))
    a_all.start(lambda d: sas.at[d, pl.ds(0, 64)])
    b_all.start(lambda d: sas.at[d, pl.ds(64, 64)])
    f_sends = []
    for k in (4, 5, 3, 2, 6, 7, 1):
        other = tr(k)
        send = remote(folded.at[other], frows.at[t], f_snd.at[k - 1], f_rcv.at[t], other, sigma)
        send.start()
        f_sends.append(send)
    sa[2 * x + c] = sas[c, 0:64, :]
    sb[2 * z + c] = sas[c, 64:128, :]
    sat[c, 2 * y] = sas[0]
    sat[c, 2 * y + 1] = sas[1]

    for k in range(2, 8):
        j = lax.rem(2 * y + k, 8)
        sat[c, j] = adjoint(j)
    sat_send = remote(sat.at[c], sat.at[c], st_snd, st_rcv, partner, sigma)
    sat_send.start()

    a_all.forward()
    b_all.forward()

    for k in range(1, 4):
        src = lax.rem(z + k, 4)
        remote(faz.at[z], faz.at[src], fz_snd.at[k - 1], fz_rcv.at[src], t, zpeer(k)).wait_recv()
    phi_of(faz, 1, phb_h, phb_l)

    low_lanes = iota((32, 128), 1) < 64

    def gradient(slots, out_h, out_l, dest):
        total = jnp.zeros((64, 256), F32)
        for q in range(4):
            high, low = halves(jnp.concatenate([slots[2 * q], slots[2 * q + 1]], axis=1))
            total = total + mm(high, out_h[q]) + mm(low, out_h[q]) + mm(high, out_l[q])
        for pair in range(2):
            top = total[0:32, 128 * pair:128 * pair + 128]
            bottom = total[32:64, 128 * pair:128 * pair + 128]
            dest[2 * pair] = jnp.where(low_lanes, top, pltpu.roll(bottom, 64, 1))
            dest[2 * pair + 1] = jnp.where(low_lanes, pltpu.roll(top, 64, 1), bottom)

    g_sends = []
    a_all.finish()
    gradient(sa, pha_h, pha_l, ga)
    for k in (2, 1, 3):
        send = remote(ga.at[lax.rem(z + k, 4)], gra.at[z], ga_snd.at[k - 1], ga_rcv.at[z], t, zpeer(k))
        send.start()
        g_sends.append(send)
    b_all.finish()
    gradient(sb, phb_h, phb_l, gb)
    for k in (2, 1, 3):
        send = remote(gb.at[lax.rem(x + k, 4)], grb.at[x], gb_snd.at[k - 1], gb_rcv.at[x], t, xpeer(k))
        send.start()
        g_sends.append(send)
    gra[z] = ga[z]
    grb[x] = gb[x]

    for i in range(8):
        ownp[:, 128 * i:128 * i + 128] = onehot(iota((256, 128), 0) + 256 * y == party[i])
    wide = mm(ownp[...], ehl[...])
    for d in range(2):
        first = pl.multiple_of(256 * y + 128 * d, 128)
        limit = upright(thr_ref[:, pl.ds(first, 128)])
        soft = jax.nn.softplus(wide[128 * d:128 * d + 128, :128] + wide[128 * d:128 * d + 128, 128:] - limit)
        xs[d] = jnp.broadcast_to(jnp.sum(soft.T, axis=0, keepdims=True), (8, 128))
    x_sends = []
    for k in range(0, 4):
        for e in range(2):
            if k == 0 and e == 0:
                continue
            d = lax.rem(c + e, 2)
            send = remote(xs.at[d], xr.at[2 * x + c], x_snd.at[2 * k + e - 1], x_rcv.at[2 * x + c], 2 * y + d, xpeer(k))
            send.start()
            x_sends.append(send)
    xr[2 * x + c] = xs[c]

    for k in range(1, 8):
        src = tr(k)
        remote(folded.at[0], frows.at[src], f_snd.at[k - 1], f_rcv.at[src], src, sigma).wait_recv()
    remote(sat.at[c], sat.at[1 - c], st_snd, st_rcv, partner, sigma).wait_recv()
    both = jnp.zeros((128, 256), F32)
    for j in range(4):
        left_h, left_l = halves(jnp.concatenate([frows[2 * j], frows[2 * j + 1]], axis=1))
        right = [jnp.concatenate([sat[0, 2 * j + i], sat[1, 2 * j + i]], axis=1) for i in range(2)]
        right_h, right_l = halves(jnp.concatenate(right, axis=0))
        both = both + mm(left_h, right_h) + mm(left_l, right_h) + mm(left_h, right_l)
    feat_out[...] = both

    for k in range(0, 4):
        for e in range(2):
            if k == 0 and e == 0:
                continue
            d = lax.rem(c + e, 2)
            slot = 2 * lax.rem(x + k, 4) + d
            remote(xr.at[slot], xr.at[slot], x_snd.at[2 * k + e - 1], x_rcv.at[slot], 2 * y + d, xpeer(k)).wait_recv()
    part = xr[0]
    for j in range(1, 8):
        part = part + xr[j]
    xt[...] = part
    for k in range(1, 4):
        send = remote(xt, xz.at[z], x2_snd.at[k - 1], x2_rcv.at[z], t, zpeer(k))
        send.start()
        x_sends.append(send)
    xz[z] = part

    row = iota((128, 128), 0)
    of_row = (row // 64) * 32 + ((row % 64) // 32) * 64 + row % 32 + 128 * t
    for j in range(16):
        memt[:, 128 * j:128 * j + 128] = onehot(of_row == sot_ref[:, 128 * j:128 * j + 128])

    for k in range(1, 4):
        src = lax.rem(z + k, 4)
        remote(ga.at[0], gra.at[src], ga_snd.at[k - 1], ga_rcv.at[src], t, zpeer(k)).wait_recv()
    for k in range(1, 4):
        src = lax.rem(x + k, 4)
        remote(gb.at[0], grb.at[src], gb_snd.at[k - 1], gb_rcv.at[src], t, xpeer(k)).wait_recv()
    grad_a = (gra[0] + gra[1]) + (gra[2] + gra[3])
    grad_b = (grb[0] + grb[1]) + (grb[2] + grb[3])
    grads = (jnp.concatenate([grad_a, grad_b], axis=0) * (1.0 / SCEN)).T
    high, low = halves(grads)
    even, odd = memt[0:64, :], memt[64:128, :]
    coef_out[...] = (mm(high[0:64], even) + mm(low[0:64], even)) + (mm(high[64:128], odd) + mm(low[64:128], odd))

    for k in range(1, 4):
        src = lax.rem(z + k, 4)
        remote(xt, xz.at[src], x2_snd.at[k - 1], x2_rcv.at[src], t, zpeer(k)).wait_recv()
    whole = (xz[0] + xz[1]) + (xz[2] + xz[3])
    first = pl.multiple_of(128 * t, 128)
    xva_out[...] = w_ref[:, pl.ds(first, 128)] * whole[0:1, :] * (1.0 / SCEN)

    for send in party_sends + fac_sends + e_all.sends + f_sends + a_all.sends + b_all.sends + [sat_send] + x_sends + g_sends:
        send.wait_send()


def place_outputs(xva, coef, feat, xva_out, coef_out, feat_out, sem):
    copies = []
    for i, (src, dst) in enumerate(((coef, coef_out), (feat, feat_out), (xva, xva_out))):
        copy = pltpu.make_async_copy(src, dst, sem.at[i])
        copy.start()
        copies.append(copy)
    for copy in copies:
        copy.wait()


def local(factors, feat_factor, feat_degree, coefficients, set_of_trade, party_of_set, threshold, weight):
    vmem = pl.BlockSpec(memory_space=pltpu.VMEM)
    hbm = pl.BlockSpec(memory_space=pltpu.HBM)
    V = pltpu.VMEM
    D = pltpu.SemaphoreType.DMA
    scratch = [
        V((1, 1024), jnp.int32), V((1, 1024), jnp.int32), V((1, 2048), jnp.int32),
        V((1, 128), jnp.int32), V((1, 1024), F32), V((1, 1024), F32),
        V((1024, 2048), F32),
        V((2048, 128), BF),
        V((128, 2048), BF),
        V((2, 768, 256), BF),
        V((256, 128), F32),
        V((256, 768), BF), V((256, 768), BF),
        V((4, 64, 256), F32), V((4, 64, 256), F32),
        V((4, 256, 256), BF), V((4, 256, 256), BF), V((4, 256, 256), BF), V((4, 256, 256), BF),
        V((8, 128, 128), F32),
        V((768, 128), F32),
        V((8, 128, 128), F32),
        V((2, 128, 128), F32),
        V((8, 128, 128), F32),
        V((1024, 256), BF),
        V((8, 1, 128), jnp.int32),
        V((8, 128, 128), F32),
        V((1024, 1024), BF),
        V((256, 1024), BF),
        V((8, 128, 8), F32),
        V((2, 128, 128), F32),
        V((8, 64, 128), F32), V((8, 64, 128), F32),
        V((2, 8, 128, 128), F32),
        V((2, 8, 128), F32), V((8, 8, 128), F32), V((8, 128), F32), V((4, 8, 128), F32),
        V((4, 32, 128), F32), V((4, 32, 128), F32), V((4, 32, 128), F32), V((4, 32, 128), F32),
        D((8,)), D((8,)), D((7,)), D((8,)), D((3,)), D((4,)), D((3,)), D((4,)), D((7,)), D((8,)), D((7,)), D((8,)),
        D((7,)), D((8,)), D((7,)), D((8,)), D(()), D(()), D((7,)), D((8,)), D((3,)), D((4,)),
        D((3,)), D((4,)), D((3,)), D((4,)),
    ]
    shapes = (
        jax.ShapeDtypeStruct((1, 128), F32),
        jax.ShapeDtypeStruct((64, 2048), F32),
        jax.ShapeDtypeStruct((128, 256), F32),
    )
    results = pl.pallas_call(
        kernel,
        out_shape=shapes,
        in_specs=[hbm] * 8,
        out_specs=(vmem, vmem, vmem),
        scratch_shapes=scratch,
        compiler_params=pltpu.CompilerParams(collective_id=0, has_side_effects=True, vmem_limit_bytes=40 << 20),
    )(*[
        pltpu.with_memory_space_constraint(array, pltpu.HBM)
        for array in (
            coefficients, factors.T, feat_factor.reshape(1, -1), feat_degree.reshape(1, -1),
            set_of_trade.reshape(1, -1), party_of_set.reshape(1, -1), threshold.reshape(1, -1), weight.reshape(1, -1),
        )
    ])
    xva, coef_sens, feature_sens = pl.pallas_call(
        place_outputs,
        out_shape=shapes,
        in_specs=[vmem] * 3,
        out_specs=(hbm, hbm, hbm),
        scratch_shapes=[D((3,))],
        compiler_params=pltpu.CompilerParams(vmem_limit_bytes=4 << 20),
    )(*results)
    return xva.reshape(-1), coef_sens, feature_sens


def solution(mesh):
    placed = (P("scen", None), P(), P(), P(None, "trade"), P("trade"), P("trade"), P(), P())
    return jax.shard_map(
        local,
        mesh=mesh,
        in_specs=placed,
        out_specs=(P("trade"), P("scen", "trade"), P("trade", "scen")),
        check_vma=False,
    )
```

time: 40.5 us -> 42.9 us (1.059)
  Pallas kernels: 32.5 us -> 42.1 us
  local copies, waits for them, and re-layouts: 6.99 us -> 0 us
    pallas_call x1 -> x2, Pallas kernels: 32.5 us -> 42.1 us  [the longest x1 41.2 us: local(): pl.pallas_call(kernel, out_shape=shapes, in_specs=[hbm] * 8, out_specs=(v...]
    unnamed x16 -> x0, local copies, waits for them, and re-layouts: 6.99 us -> none
where the time goes in v2:
time: 42.9 us; the launch traced here: 42.7 us
  Pallas kernels  42.1 us (98%)
  between operations  0.64 us (1%)
    pallas_call x1, Pallas kernels, local(): pl.pallas_call(kernel, out_shape=shapes, in_specs=[hbm] * 8, out_specs=(v...  41.2 us
    pallas_call x1, Pallas kernels, local(): pl.pallas_call(place_outputs, out_shape=shapes, in_specs=[vmem] * 3, out_...  0.86 us

profile of v2, /device:TPU:0, one launch (start us, length us, event | category | flops | bytes accessed | tf_op | source)
XLA Modules:
  0.0 42.7 jit_solution(13334110863536236064)
XLA Ops:
  0.6 41.2 %shard_map.103 = (f32[1,128]{1,0:T(1,128)S(1)}, f32[64,2048]{1,0:T(8,128)S(1)}, f32[128,256]{1,0:T(8,128)S(1)}) custom-call(f32[1024,2048]{1,0:T(8,128)} %coef_hbm.1, f32[64,256]{1,0:T(8,128)} %bitcast.8, s32[1,1024]{1,0:T(1,128)} %bitcast.10, s32[1,1024]{1,0:T(1,128)} %bitcast.11, s32[1,2048]{1,0:T(1,128)} %bitcast.9, s32[1,128]{1,0:T(1,128)} %bitcast.14, ...), custom_call_target="tpu_custom_call" | custom-call | tf_op jit(solution)/shard_map/pallas_call | solution.py:458
  41.8 0.9 %shard_map.104 = (f32[1,128]{1,0:T(1,128)}, f32[64,2048]{1,0:T(8,128)}, f32[128,256]{1,0:T(8,128)}) custom-call(f32[1,128]{1,0:T(1,128)S(1)} %get-tuple-element.9.xva, f32[64,2048]{1,0:T(8,128)S(1)} %get-tuple-element.10.coef, f32[128,256]{1,0:T(8,128)S(1)} %get-tuple-element.11.feat), custom_call_target="tpu_custom_call" | custom-call | tf_op jit(solution)/shard_map/pallas_call | solution.py:472

commit v3 on v2

--- a/solution.py
+++ b/solution.py
@@ -63,8 +63,8 @@
     coef_hbm, fac_hbm, ff_hbm, fd_hbm, sot_hbm, pos_hbm, thr_hbm, w_hbm,
     xva_out, coef_out, feat_out,
     ff_ref, fd_ref, sot_ref, pos_ref, thr_ref, w_ref, cbuf,
-    member, memt, pick, dup, th, tl, fax, faz, pha_h, pha_l, phb_h, phb_l,
-    folded, gsum, frows, etb, eh, ehl, party, pcol, same, ownp, tw, sas, sa, sb, sat,
+    member, memt, pick, th, tl, fax, faz, pha_h, pha_l, phb_h, phb_l,
+    spot, fparts, folded, gsum, frows, etb, eh, ehl, party, pcol, same, ownp, tw, sas, sa, sb, sat,
     xs, xr, xt, xz, ga, gb, gra, grb, i_sem,
     c_sem, p_snd, p_rcv, fx_snd, fx_rcv, fz_snd, fz_rcv, e_snd, e_rcv, f_snd, f_rcv,
     sa_snd, sa_rcv, sb_snd, sb_rcv, st_snd, st_rcv, x_snd, x_rcv, x2_snd, x2_rcv,
@@ -109,6 +109,16 @@
             self.put(piece(1 - c), slot, 2, 1, 1 - c)
             self.put(piece(c), slot, 3, 3, c)
             self.put(piece(1 - c), slot, 4, 0, 1 - c)
+
+        def start_direct(self, piece):
+            slot = 2 * self.mine + c
+            for i, (k, e) in enumerate(((2, 0), (2, 1), (1, 0), (3, 0), (1, 1), (3, 1), (0, 1))):
+                d = lax.rem(c + e, 2)
+                self.put(piece(d), slot, i, k, d)
+
+        def finish_direct(self):
+            for k, e in ((0, 1), (3, 0), (3, 1), (1, 0), (1, 1), (2, 0), (2, 1)):
+                self.wait_slot(k, e)
 
         def wait_slot(self, k, e):
             slot = 2 * lax.rem(self.mine + k, 4) + lax.rem(c + e, 2)
@@ -137,10 +147,9 @@
     loads = []
     for i in range(8):
         rows = pl.ds(128 * i, 128)
-        load = pltpu.make_async_copy(coef_hbm.at[rows], cbuf.at[rows], c_sem.at[i])
+        loads.append(pltpu.make_async_copy(coef_hbm.at[rows], cbuf.at[rows], c_sem.at[i]))
+    for load in loads[:2]:
         load.start()
-        loads.append(load)
-
     barrier = pltpu.get_barrier_semaphore()
     for k in range(1, 8):
         pl.semaphore_signal(barrier, inc=1, device_id=(tr(k), sigma), device_id_type=MESH)
@@ -151,6 +160,8 @@
 
     for small in smalls:
         small.wait()
+    for load in loads[2:]:
+        load.start()
 
     base = (128 * t).astype(F32)
     lanes = iota((128, 128), 1).astype(F32)
@@ -164,6 +175,15 @@
     degree_basis(doubled(fax[x]), th, tl)
 
     keys = (fd_ref[...] - 1) * 64 + ff_ref[...]
+    for i in range(8):
+        cols = slice(128 * i, 128 * i + 128)
+        spot[:, cols] = onehot(iota((768, 128), 0) == keys[:, cols])
+
+    def regroup(i):
+        rows = slice(256 * i, 256 * i + 256)
+        wide = mm(spot[:, rows], fparts[rows, :])
+        return wide[:, :128] + wide[:, 128:]
+
     for i in range(4):
         loads[2 * i].wait()
         loads[2 * i + 1].wait()
@@ -172,40 +192,38 @@
         fold = mm(high, member[...]) + mm(low, member[...])
         folded[2 * i] = fold[:128, :]
         folded[2 * i + 1] = fold[128:, :]
-        spot = onehot(iota((768, 256), 0) == keys[:, rows])
-        wide = mm(spot, jnp.concatenate(halves(fold), axis=1))
-        wide = wide[:, :128] + wide[:, 128:]
-        if i == 0:
-            gsum[...] = wide
-        elif i < 3:
-            gsum[...] += wide
-        else:
-            total = gsum[...] + wide
-    high, low = halves(total)
+        high, low = halves(fold)
+        fparts[rows, 0:128] = high
+        fparts[rows, 128:256] = low
+        if i == 1:
+            gsum[...] = regroup(0)
+        elif i > 1:
+            gsum[...] += regroup(i - 1)
+        if i == 1:
+            pl.semaphore_wait(barrier, 19)
+            party_sends = []
+            for k in range(1, 8):
+                send = remote(pos_ref, party.at[t], p_snd.at[k - 1], p_rcv.at[t], tr(k), sigma)
+                send.start()
+                party_sends.append(send)
+            fac_sends = []
+            for k in range(1, 4):
+                send = remote(fax.at[x], fax.at[x], fx_snd.at[k - 1], fx_rcv.at[x], t, xpeer(k))
+                send.start()
+                fac_sends.append(send)
+                send = remote(faz.at[z], faz.at[z], fz_snd.at[k - 1], fz_rcv.at[z], t, zpeer(k))
+                send.start()
+                fac_sends.append(send)
+            party[t] = pos_ref[...]
+    high, low = halves(gsum[...] + regroup(3))
     wide = mm(th[...], jnp.concatenate([high, low], axis=1))
     exposure = wide[:, :128] + wide[:, 128:] + mm(tl[...], high)
     etb[0] = exposure[0:128, :].T
     etb[1] = exposure[128:256, :].T
 
-    pl.semaphore_wait(barrier, 19)
-
     e_all = Gather(eh, e_snd, e_rcv, y, lambda k, d: (2 * lax.rem(y + k, 4) + d, sigma))
     e_all.start(lambda d: etb.at[d])
 
-    party_sends = []
-    for k in range(1, 8):
-        send = remote(pos_ref, party.at[t], p_snd.at[k - 1], p_rcv.at[t], tr(k), sigma)
-        send.start()
-        party_sends.append(send)
-    fac_sends = []
-    for k in range(1, 4):
-        send = remote(fax.at[x], fax.at[x], fx_snd.at[k - 1], fx_rcv.at[x], t, xpeer(k))
-        send.start()
-        fac_sends.append(send)
-        send = remote(faz.at[z], faz.at[z], fz_snd.at[k - 1], fz_rcv.at[z], t, zpeer(k))
-        send.start()
-        fac_sends.append(send)
-    party[t] = pos_ref[...]
     eh[t] = etb[c]
     frows[t] = folded[t]
 
@@ -271,8 +289,8 @@
 
     a_all = Gather(sa, sa_snd, sa_rcv, x, lambda k, d: (2 * y + d, xpeer(k)))
     b_all = Gather(sb, sb_snd, sb_rcv, z, lambda k, d: (2 * y + d, zpeer(k)))
-    a_all.start(lambda d: sas.at[d, pl.ds(0, 64)])
-    b_all.start(lambda d: sas.at[d, pl.ds(64, 64)])
+    a_all.start_direct(lambda d: sas.at[d, pl.ds(0, 64)])
+    b_all.start_direct(lambda d: sas.at[d, pl.ds(64, 64)])
     f_sends = []
     for k in (4, 5, 3, 2, 6, 7, 1):
         other = tr(k)
@@ -289,43 +307,6 @@
         sat[c, j] = adjoint(j)
     sat_send = remote(sat.at[c], sat.at[c], st_snd, st_rcv, partner, sigma)
     sat_send.start()
-
-    a_all.forward()
-    b_all.forward()
-
-    for k in range(1, 4):
-        src = lax.rem(z + k, 4)
-        remote(faz.at[z], faz.at[src], fz_snd.at[k - 1], fz_rcv.at[src], t, zpeer(k)).wait_recv()
-    phi_of(faz, 1, phb_h, phb_l)
-
-    low_lanes = iota((32, 128), 1) < 64
-
-    def gradient(slots, out_h, out_l, dest):
-        total = jnp.zeros((64, 256), F32)
-        for q in range(4):
-            high, low = halves(jnp.concatenate([slots[2 * q], slots[2 * q + 1]], axis=1))
-            total = total + mm(high, out_h[q]) + mm(low, out_h[q]) + mm(high, out_l[q])
-        for pair in range(2):
-            top = total[0:32, 128 * pair:128 * pair + 128]
-            bottom = total[32:64, 128 * pair:128 * pair + 128]
-            dest[2 * pair] = jnp.where(low_lanes, top, pltpu.roll(bottom, 64, 1))
-            dest[2 * pair + 1] = jnp.where(low_lanes, pltpu.roll(top, 64, 1), bottom)
-
-    g_sends = []
-    a_all.finish()
-    gradient(sa, pha_h, pha_l, ga)
-    for k in (2, 1, 3):
-        send = remote(ga.at[lax.rem(z + k, 4)], gra.at[z], ga_snd.at[k - 1], ga_rcv.at[z], t, zpeer(k))
-        send.start()
-        g_sends.append(send)
-    b_all.finish()
-    gradient(sb, phb_h, phb_l, gb)
-    for k in (2, 1, 3):
-        send = remote(gb.at[lax.rem(x + k, 4)], grb.at[x], gb_snd.at[k - 1], gb_rcv.at[x], t, xpeer(k))
-        send.start()
-        g_sends.append(send)
-    gra[z] = ga[z]
-    grb[x] = gb[x]
 
     for i in range(8):
         ownp[:, 128 * i:128 * i + 128] = onehot(iota((256, 128), 0) + 256 * y == party[i])
@@ -346,6 +327,57 @@
             x_sends.append(send)
     xr[2 * x + c] = xs[c]
 
+    for k in range(1, 4):
+        src = lax.rem(z + k, 4)
+        remote(faz.at[z], faz.at[src], fz_snd.at[k - 1], fz_rcv.at[src], t, zpeer(k)).wait_recv()
+    phi_of(faz, 1, phb_h, phb_l)
+
+    low_lanes = iota((32, 128), 1) < 64
+
+    def gradient(slots, out_h, out_l, dest):
+        total = jnp.zeros((64, 256), F32)
+        for q in range(4):
+            high, low = halves(jnp.concatenate([slots[2 * q], slots[2 * q + 1]], axis=1))
+            total = total + mm(high, out_h[q]) + mm(low, out_h[q]) + mm(high, out_l[q])
+        for pair in range(2):
+            top = total[0:32, 128 * pair:128 * pair + 128]
+            bottom = total[32:64, 128 * pair:128 * pair + 128]
+            dest[2 * pair] = jnp.where(low_lanes, top, pltpu.roll(bottom, 64, 1))
+            dest[2 * pair + 1] = jnp.where(low_lanes, pltpu.roll(top, 64, 1), bottom)
+
+    g_sends = []
+    a_all.finish_direct()
+    gradient(sa, pha_h, pha_l, ga)
+    for k in (2, 1, 3):
+        send = remote(ga.at[lax.rem(z + k, 4)], gra.at[z], ga_snd.at[k - 1], ga_rcv.at[z], t, zpeer(k))
+        send.start()
+        g_sends.append(send)
+    b_all.finish_direct()
+    gradient(sb, phb_h, phb_l, gb)
+    for k in (2, 1, 3):
+        send = remote(gb.at[lax.rem(x + k, 4)], grb.at[x], gb_snd.at[k - 1], gb_rcv.at[x], t, xpeer(k))
+        send.start()
+        g_sends.append(send)
+    gra[z] = ga[z]
+    grb[x] = gb[x]
+
+    for k in range(0, 4):
+        for e in range(2):
+            if k == 0 and e == 0:
+                continue
+            d = lax.rem(c + e, 2)
+            slot = 2 * lax.rem(x + k, 4) + d
+            remote(xr.at[slot], xr.at[slot], x_snd.at[2 * k + e - 1], x_rcv.at[slot], 2 * y + d, xpeer(k)).wait_recv()
+    part = xr[0]
+    for j in range(1, 8):
+        part = part + xr[j]
+    xt[...] = part
+    for k in range(1, 4):
+        send = remote(xt, xz.at[z], x2_snd.at[k - 1], x2_rcv.at[z], t, zpeer(k))
+        send.start()
+        x_sends.append(send)
+    xz[z] = part
+
     for k in range(1, 8):
         src = tr(k)
         remote(folded.at[0], frows.at[src], f_snd.at[k - 1], f_rcv.at[src], src, sigma).wait_recv()
@@ -357,23 +389,6 @@
         right_h, right_l = halves(jnp.concatenate(right, axis=0))
         both = both + mm(left_h, right_h) + mm(left_l, right_h) + mm(left_h, right_l)
     feat_out[...] = both
-
-    for k in range(0, 4):
-        for e in range(2):
-            if k == 0 and e == 0:
-                continue
-            d = lax.rem(c + e, 2)
-            slot = 2 * lax.rem(x + k, 4) + d
-            remote(xr.at[slot], xr.at[slot], x_snd.at[2 * k + e - 1], x_rcv.at[slot], 2 * y + d, xpeer(k)).wait_recv()
-    part = xr[0]
-    for j in range(1, 8):
-        part = part + xr[j]
-    xt[...] = part
-    for k in range(1, 4):
-        send = remote(xt, xz.at[z], x2_snd.at[k - 1], x2_rcv.at[z], t, zpeer(k))
-        send.start()
-        x_sends.append(send)
-    xz[z] = part
 
     row = iota((128, 128), 0)
     of_row = (row // 64) * 32 + ((row % 64) // 32) * 64 + row % 32 + 128 * t
@@ -426,10 +441,11 @@
         V((2048, 128), BF),
         V((128, 2048), BF),
         V((2, 768, 256), BF),
-        V((256, 128), F32),
         V((256, 768), BF), V((256, 768), BF),
         V((4, 64, 256), F32), V((4, 64, 256), F32),
         V((4, 256, 256), BF), V((4, 256, 256), BF), V((4, 256, 256), BF), V((4, 256, 256), BF),
+        V((768, 1024), BF),
+        V((1024, 256), BF),
         V((8, 128, 128), F32),
         V((768, 128), F32),
         V((8, 128, 128), F32),

time: 42.9 us -> 32.9 us (0.77)
  the two profiles are of different devices: /device:TPU:0 before, /device:TPU:1 now
where the time goes in v3:
time: 32.9 us; the launch traced here: 32.7 us
  Pallas kernels  32.1 us (98%)
  between operations  0.64 us (2%)
    pallas_call x1, Pallas kernels, local(): pl.pallas_call(kernel, out_shape=shapes, in_specs=[hbm] * 8, out_specs=(v...  31.2 us
    pallas_call x1, Pallas kernels, local(): pl.pallas_call(place_outputs, out_shape=shapes, in_specs=[vmem] * 3, out_...  0.86 us

profile of v3, /device:TPU:1, one launch (start us, length us, event | category | flops | bytes accessed | tf_op | source)
XLA Modules:
  0.0 32.7 jit_solution(7668445720289566529)
XLA Ops:
  0.6 31.2 %shard_map.103 = (f32[1,128]{1,0:T(1,128)S(1)}, f32[64,2048]{1,0:T(8,128)S(1)}, f32[128,256]{1,0:T(8,128)S(1)}) custom-call(f32[1024,2048]{1,0:T(8,128)} %coef_hbm.1, f32[64,256]{1,0:T(8,128)} %bitcast.8, s32[1,1024]{1,0:T(1,128)} %bitcast.10, s32[1,1024]{1,0:T(1,128)} %bitcast.11, s32[1,2048]{1,0:T(1,128)} %bitcast.9, s32[1,128]{1,0:T(1,128)} %bitcast.14, ...), custom_call_target="tpu_custom_call" | custom-call | tf_op jit(solution)/shard_map/pallas_call | solution.py:474
  31.9 0.9 %shard_map.104 = (f32[1,128]{1,0:T(1,128)}, f32[64,2048]{1,0:T(8,128)}, f32[128,256]{1,0:T(8,128)}) custom-call(f32[1,128]{1,0:T(1,128)S(1)} %get-tuple-element.9.xva, f32[64,2048]{1,0:T(8,128)S(1)} %get-tuple-element.10.coef, f32[128,256]{1,0:T(8,128)S(1)} %get-tuple-element.11.feat), custom_call_target="tpu_custom_call" | custom-call | tf_op jit(solution)/shard_map/pallas_call | solution.py:488

commit v4 on v3

--- a/solution.py
+++ b/solution.py
@@ -64,7 +64,7 @@
     xva_out, coef_out, feat_out,
     ff_ref, fd_ref, sot_ref, pos_ref, thr_ref, w_ref, cbuf,
     member, memt, pick, th, tl, fax, faz, pha_h, pha_l, phb_h, phb_l,
-    spot, fparts, folded, gsum, frows, etb, eh, ehl, party, pcol, same, ownp, tw, sas, sa, sb, sat,
+    spot, fparts, folded, frows, etb, eh, ehl, party, pcol, same, ownp, tw, sas, sa, sb, sat,
     xs, xr, xt, xz, ga, gb, gra, grb, i_sem,
     c_sem, p_snd, p_rcv, fx_snd, fx_rcv, fz_snd, fz_rcv, e_snd, e_rcv, f_snd, f_rcv,
     sa_snd, sa_rcv, sb_snd, sb_rcv, st_snd, st_rcv, x_snd, x_rcv, x2_snd, x2_rcv,
@@ -102,39 +102,54 @@
             send.start()
             self.sends.append(send)
 
-        def start(self, piece):
+        def start(self, src, e):
+            d = lax.rem(c + e, 2)
+            for i, k in enumerate((2, 1, 3) + (() if e == 0 else (0,))):
+                self.put(src, 2 * self.mine + c, 4 * e + i, k, d)
+
+        def wait(self, k):
+            for e in range(2):
+                if k or e:
+                    slot = 2 * lax.rem(self.mine + k, 4) + lax.rem(c + e, 2)
+                    trade, scen = self.place(k, lax.rem(c + e, 2))
+                    here = self.slots.at[slot]
+                    remote(here, here, self.snd.at[0], self.rcv.at[slot], trade, scen).wait_recv()
+
+    class Relay(Gather):
+        def half(self, slot, h):
+            return self.slots.at[slot, pl.ds(64 * h, 64)]
+
+        def put(self, src, slot, i, k, d, h):
+            trade, scen = self.place(k, d)
+            send = remote(src, self.half(slot, h), self.snd.at[i], self.rcv.at[2 * slot + h], trade, scen)
+            send.start()
+            self.sends.append(send)
+
+        def start(self, src):
             slot = 2 * self.mine + c
-            self.put(piece(c), slot, 0, 1, c)
-            self.put(piece(1 - c), slot, 1, 3, 1 - c)
-            self.put(piece(1 - c), slot, 2, 1, 1 - c)
-            self.put(piece(c), slot, 3, 3, c)
-            self.put(piece(1 - c), slot, 4, 0, 1 - c)
-
-        def start_direct(self, piece):
-            slot = 2 * self.mine + c
-            for i, (k, e) in enumerate(((2, 0), (2, 1), (1, 0), (3, 0), (1, 1), (3, 1), (0, 1))):
+            for i, (k, e) in enumerate(((1, 0), (3, 1), (1, 1), (3, 0), (0, 1))):
                 d = lax.rem(c + e, 2)
-                self.put(piece(d), slot, i, k, d)
-
-        def finish_direct(self):
-            for k, e in ((0, 1), (3, 0), (3, 1), (1, 0), (1, 1), (2, 0), (2, 1)):
-                self.wait_slot(k, e)
-
-        def wait_slot(self, k, e):
+                for h in range(2):
+                    self.put(src.at[d, pl.ds(64 * h, 64)], slot, 2 * i + h, k, d, h)
+
+        def wait(self, k, e, h):
             slot = 2 * lax.rem(self.mine + k, 4) + lax.rem(c + e, 2)
-            trade, scen = self.place(k, lax.rem(c + e, 2)) if k or e else self.place(0, 1 - c)
-            remote(self.slots.at[slot], self.slots.at[slot], self.snd.at[0], self.rcv.at[slot], trade, scen).wait_recv()
+            trade, scen = self.place(k if k else 0, lax.rem(c + e, 2))
+            here = self.half(slot, h)
+            remote(here, here, self.snd.at[0], self.rcv.at[2 * slot + h], trade, scen).wait_recv()
             return slot
 
         def forward(self):
-            slot = self.wait_slot(3, 0)
-            self.put(self.slots.at[slot], slot, 5, 1, c)
-            slot = self.wait_slot(1, 1)
-            self.put(self.slots.at[slot], slot, 6, 3, c)
+            for h in range(2):
+                slot = self.wait(3, 0, h)
+                self.put(self.half(slot, h), slot, 10 + h, 1, c, h)
+                slot = self.wait(1, 1, h)
+                self.put(self.half(slot, h), slot, 12 + h, 3, c, h)
 
         def finish(self):
-            for k, e in ((0, 1), (3, 1), (1, 0), (2, 0), (2, 1)):
-                self.wait_slot(k, e)
+            for h in range(2):
+                for k, e in ((0, 1), (3, 1), (1, 0), (2, 0), (2, 1)):
+                    self.wait(k, e, h)
 
     smalls = []
     for i, (src, dst) in enumerate((
@@ -148,8 +163,8 @@
     for i in range(8):
         rows = pl.ds(128 * i, 128)
         loads.append(pltpu.make_async_copy(coef_hbm.at[rows], cbuf.at[rows], c_sem.at[i]))
-    for load in loads[:2]:
-        load.start()
+    for load in loads:
+        load.start(priority=1)
     barrier = pltpu.get_barrier_semaphore()
     for k in range(1, 8):
         pl.semaphore_signal(barrier, inc=1, device_id=(tr(k), sigma), device_id_type=MESH)
@@ -160,9 +175,6 @@
 
     for small in smalls:
         small.wait()
-    for load in loads[2:]:
-        load.start()
-
     base = (128 * t).astype(F32)
     lanes = iota((128, 128), 1).astype(F32)
     for j in range(16):
@@ -179,14 +191,7 @@
         cols = slice(128 * i, 128 * i + 128)
         spot[:, cols] = onehot(iota((768, 128), 0) == keys[:, cols])
 
-    def regroup(i):
-        rows = slice(256 * i, 256 * i + 256)
-        wide = mm(spot[:, rows], fparts[rows, :])
-        return wide[:, :128] + wide[:, 128:]
-
-    for i in range(4):
-        loads[2 * i].wait()
-        loads[2 * i + 1].wait()
+    def fold_rows(i):
         rows = slice(256 * i, 256 * i + 256)
         high, low = halves(cbuf[rows, :])
         fold = mm(high, member[...]) + mm(low, member[...])
@@ -195,34 +200,41 @@
         high, low = halves(fold)
         fparts[rows, 0:128] = high
         fparts[rows, 128:256] = low
-        if i == 1:
-            gsum[...] = regroup(0)
-        elif i > 1:
-            gsum[...] += regroup(i - 1)
-        if i == 1:
-            pl.semaphore_wait(barrier, 19)
-            party_sends = []
-            for k in range(1, 8):
-                send = remote(pos_ref, party.at[t], p_snd.at[k - 1], p_rcv.at[t], tr(k), sigma)
-                send.start()
-                party_sends.append(send)
-            fac_sends = []
-            for k in range(1, 4):
-                send = remote(fax.at[x], fax.at[x], fx_snd.at[k - 1], fx_rcv.at[x], t, xpeer(k))
-                send.start()
-                fac_sends.append(send)
-                send = remote(faz.at[z], faz.at[z], fz_snd.at[k - 1], fz_rcv.at[z], t, zpeer(k))
-                send.start()
-                fac_sends.append(send)
-            party[t] = pos_ref[...]
-    high, low = halves(gsum[...] + regroup(3))
+
+    for load in loads[:4]:
+        load.wait()
+    fold_rows(0)
+    fold_rows(1)
+
+    pl.semaphore_wait(barrier, 19)
+    party_sends = []
+    for k in range(1, 8):
+        send = remote(pos_ref, party.at[t], p_snd.at[k - 1], p_rcv.at[t], tr(k), sigma)
+        send.start()
+        party_sends.append(send)
+    fac_sends = []
+    for k in range(1, 4):
+        send = remote(fax.at[x], fax.at[x], fx_snd.at[k - 1], fx_rcv.at[x], t, xpeer(k))
+        send.start()
+        fac_sends.append(send)
+        send = remote(faz.at[z], faz.at[z], fz_snd.at[k - 1], fz_rcv.at[z], t, zpeer(k))
+        send.start()
+        fac_sends.append(send)
+    party[t] = pos_ref[...]
+
+    for load in loads[4:]:
+        load.wait()
+    fold_rows(2)
+    fold_rows(3)
+    wide = mm(spot[...], fparts[...])
+    high, low = halves(wide[:, :128] + wide[:, 128:])
     wide = mm(th[...], jnp.concatenate([high, low], axis=1))
     exposure = wide[:, :128] + wide[:, 128:] + mm(tl[...], high)
     etb[0] = exposure[0:128, :].T
     etb[1] = exposure[128:256, :].T
 
-    e_all = Gather(eh, e_snd, e_rcv, y, lambda k, d: (2 * lax.rem(y + k, 4) + d, sigma))
-    e_all.start(lambda d: etb.at[d])
+    e_all = Relay(eh, e_snd, e_rcv, y, lambda k, d: (2 * lax.rem(y + k, 4) + d, sigma))
+    e_all.start(etb)
 
     eh[t] = etb[c]
     frows[t] = folded[t]
@@ -276,7 +288,7 @@
         ehl[128 * j:128 * j + 128, 0:128] = high
         ehl[128 * j:128 * j + 128, 128:256] = low
 
-    def adjoint(j, blocks=1):
+    def adjoint(j):
         rows = pl.ds(pl.multiple_of(j * 128, 128), 128)
         wide = mm(same[rows, :], ehl[...])
         consts = tw[j]
@@ -284,13 +296,14 @@
         scale = consts[:, 3:4] + consts[:, 4:5] + consts[:, 5:6]
         return scale * jax.nn.sigmoid(wide[:, :128] + wide[:, 128:] - shift)
 
+    a_all = Gather(sa, sa_snd, sa_rcv, x, lambda k, d: (2 * y + d, xpeer(k)))
+    b_all = Gather(sb, sb_snd, sb_rcv, z, lambda k, d: (2 * y + d, zpeer(k)))
     for d in range(2):
         sas[d] = adjoint(2 * y + d)
-
-    a_all = Gather(sa, sa_snd, sa_rcv, x, lambda k, d: (2 * y + d, xpeer(k)))
-    b_all = Gather(sb, sb_snd, sb_rcv, z, lambda k, d: (2 * y + d, zpeer(k)))
-    a_all.start_direct(lambda d: sas.at[d, pl.ds(0, 64)])
-    b_all.start_direct(lambda d: sas.at[d, pl.ds(64, 64)])
+    for e in (1, 0):
+        d = lax.rem(c + e, 2)
+        a_all.start(sas.at[d, pl.ds(0, 64)], e)
+        b_all.start(sas.at[d, pl.ds(64, 64)], e)
     f_sends = []
     for k in (4, 5, 3, 2, 6, 7, 1):
         other = tr(k)
@@ -334,27 +347,32 @@
 
     low_lanes = iota((32, 128), 1) < 64
 
-    def gradient(slots, out_h, out_l, dest):
-        total = jnp.zeros((64, 256), F32)
-        for q in range(4):
-            high, low = halves(jnp.concatenate([slots[2 * q], slots[2 * q + 1]], axis=1))
-            total = total + mm(high, out_h[q]) + mm(low, out_h[q]) + mm(high, out_l[q])
+    def gradient(slots, q, out_h, out_l):
+        high, low = halves(jnp.concatenate([slots[2 * q], slots[2 * q + 1]], axis=1))
+        both = mm(jnp.concatenate([high, low], axis=0), out_h[q])
+        return both[:64] + both[64:] + mm(high, out_l[q])
+
+    def pack(total, dest):
         for pair in range(2):
             top = total[0:32, 128 * pair:128 * pair + 128]
             bottom = total[32:64, 128 * pair:128 * pair + 128]
             dest[2 * pair] = jnp.where(low_lanes, top, pltpu.roll(bottom, 64, 1))
             dest[2 * pair + 1] = jnp.where(low_lanes, pltpu.roll(top, 64, 1), bottom)
 
+    total_a = jnp.zeros((64, 256), F32)
+    total_b = jnp.zeros((64, 256), F32)
+    for k in (0, 1, 3, 2):
+        a_all.wait(k)
+        b_all.wait(k)
+        total_a = total_a + gradient(sa, lax.rem(x + k, 4), pha_h, pha_l)
+        total_b = total_b + gradient(sb, lax.rem(z + k, 4), phb_h, phb_l)
+    pack(total_a, ga)
+    pack(total_b, gb)
     g_sends = []
-    a_all.finish_direct()
-    gradient(sa, pha_h, pha_l, ga)
     for k in (2, 1, 3):
         send = remote(ga.at[lax.rem(z + k, 4)], gra.at[z], ga_snd.at[k - 1], ga_rcv.at[z], t, zpeer(k))
         send.start()
         g_sends.append(send)
-    b_all.finish_direct()
-    gradient(sb, phb_h, phb_l, gb)
-    for k in (2, 1, 3):
         send = remote(gb.at[lax.rem(x + k, 4)], grb.at[x], gb_snd.at[k - 1], gb_rcv.at[x], t, xpeer(k))
         send.start()
         g_sends.append(send)
@@ -393,7 +411,9 @@
     row = iota((128, 128), 0)
     of_row = (row // 64) * 32 + ((row % 64) // 32) * 64 + row % 32 + 128 * t
     for j in range(16):
-        memt[:, 128 * j:128 * j + 128] = onehot(of_row == sot_ref[:, 128 * j:128 * j + 128])
+        takes = onehot(of_row == sot_ref[:, 128 * j:128 * j + 128])
+        memt[0:128, 128 * j:128 * j + 128] = takes
+        memt[128:256, 128 * j:128 * j + 128] = takes
 
     for k in range(1, 4):
         src = lax.rem(z + k, 4)
@@ -403,10 +423,9 @@
         remote(gb.at[0], grb.at[src], gb_snd.at[k - 1], gb_rcv.at[src], t, xpeer(k)).wait_recv()
     grad_a = (gra[0] + gra[1]) + (gra[2] + gra[3])
     grad_b = (grb[0] + grb[1]) + (grb[2] + grb[3])
-    grads = (jnp.concatenate([grad_a, grad_b], axis=0) * (1.0 / SCEN)).T
-    high, low = halves(grads)
-    even, odd = memt[0:64, :], memt[64:128, :]
-    coef_out[...] = (mm(high[0:64], even) + mm(low[0:64], even)) + (mm(high[64:128], odd) + mm(low[64:128], odd))
+    grads = jnp.concatenate([grad_a, grad_b], axis=0) * (1.0 / SCEN)
+    grads = jnp.concatenate([grads, pltpu.roll(grads, 64, 1)], axis=0).T[0:64, :]
+    coef_out[...] = mm(jnp.concatenate(halves(grads), axis=1), memt[...])
 
     for k in range(1, 4):
         src = lax.rem(z + k, 4)
@@ -439,7 +458,7 @@
         V((1, 128), jnp.int32), V((1, 1024), F32), V((1, 1024), F32),
         V((1024, 2048), F32),
         V((2048, 128), BF),
-        V((128, 2048), BF),
+        V((256, 2048), BF),
         V((2, 768, 256), BF),
         V((256, 768), BF), V((256, 768), BF),
         V((4, 64, 256), F32), V((4, 64, 256), F32),
@@ -447,7 +466,6 @@
         V((768, 1024), BF),
         V((1024, 256), BF),
         V((8, 128, 128), F32),
-        V((768, 128), F32),
         V((8, 128, 128), F32),
         V((2, 128, 128), F32),
         V((8, 128, 128), F32),
@@ -462,8 +480,8 @@
         V((2, 8, 128, 128), F32),
         V((2, 8, 128), F32), V((8, 8, 128), F32), V((8, 128), F32), V((4, 8, 128), F32),
         V((4, 32, 128), F32), V((4, 32, 128), F32), V((4, 32, 128), F32), V((4, 32, 128), F32),
-        D((8,)), D((8,)), D((7,)), D((8,)), D((3,)), D((4,)), D((3,)), D((4,)), D((7,)), D((8,)), D((7,)), D((8,)),
-        D((7,)), D((8,)), D((7,)), D((8,)), D(()), D(()), D((7,)), D((8,)), D((3,)), D((4,)),
+        D((8,)), D((8,)), D((7,)), D((8,)), D((3,)), D((4,)), D((3,)), D((4,)), D((14,)), D((16,)), D((7,)), D((8,)),
+        D((8,)), D((8,)), D((8,)), D((8,)), D(()), D(()), D((7,)), D((8,)), D((3,)), D((4,)),
         D((3,)), D((4,)), D((3,)), D((4,)),
     ]
     shapes = (

time: 32.9 us -> 31 us (0.942)
  the two profiles are of different devices: /device:TPU:1 before, /device:TPU:0 now
where the time goes in v4:
time: 31 us; the launch traced here: 30.9 us
  Pallas kernels  30.2 us (97%)
  between operations  0.64 us (2%)
    pallas_call x1, Pallas kernels, local(): pl.pallas_call(kernel, out_shape=shapes, in_specs=[hbm] * 8, out_specs=(v...  29.4 us
    pallas_call x1, Pallas kernels, local(): pl.pallas_call(place_outputs, out_shape=shapes, in_specs=[vmem] * 3, out_...  0.86 us

profile of v4, /device:TPU:0, one launch (start us, length us, event | category | flops | bytes accessed | tf_op | source)
XLA Modules:
  0.0 30.9 jit_solution(6409984341274346099)
XLA Ops:
  0.6 29.4 %shard_map.103 = (f32[1,128]{1,0:T(1,128)S(1)}, f32[64,2048]{1,0:T(8,128)S(1)}, f32[128,256]{1,0:T(8,128)S(1)}) custom-call(f32[1024,2048]{1,0:T(8,128)} %coef_hbm.1, f32[64,256]{1,0:T(8,128)} %bitcast.8, s32[1,1024]{1,0:T(1,128)} %bitcast.10, s32[1,1024]{1,0:T(1,128)} %bitcast.11, s32[1,2048]{1,0:T(1,128)} %bitcast.9, s32[1,128]{1,0:T(1,128)} %bitcast.14, ...), custom_call_target="tpu_custom_call" | custom-call | tf_op jit(solution)/shard_map/pallas_call | solution.py:492
  30.0 0.9 %shard_map.104 = (f32[1,128]{1,0:T(1,128)}, f32[64,2048]{1,0:T(8,128)}, f32[128,256]{1,0:T(8,128)}) custom-call(f32[1,128]{1,0:T(1,128)S(1)} %get-tuple-element.9.xva, f32[64,2048]{1,0:T(8,128)S(1)} %get-tuple-element.10.coef, f32[128,256]{1,0:T(8,128)S(1)} %get-tuple-element.11.feat), custom_call_target="tpu_custom_call" | custom-call | tf_op jit(solution)/shard_map/pallas_call | solution.py:506

commit v5 on v4

--- a/solution.py
+++ b/solution.py
@@ -61,10 +61,10 @@
 
 def kernel(
     coef_hbm, fac_hbm, ff_hbm, fd_hbm, sot_hbm, pos_hbm, thr_hbm, w_hbm,
-    xva_out, coef_out, feat_out,
+    xva_out, feat_out, grads_out, memt,
     ff_ref, fd_ref, sot_ref, pos_ref, thr_ref, w_ref, cbuf,
-    member, memt, pick, th, tl, fax, faz, pha_h, pha_l, phb_h, phb_l,
-    spot, fparts, folded, frows, etb, eh, ehl, party, pcol, same, ownp, tw, sas, sa, sb, sat,
+    member, pick, th, tl, tph, tpl, fax, faz, pha_h, pha_l, phb_h, phb_l,
+    spot, fparts, folded, frows, etb, eh, ehl, party, pcol, same, ownp, tw, lims, sas, sa, sb, sat,
     xs, xr, xt, xz, ga, gb, gra, grb, i_sem,
     c_sem, p_snd, p_rcv, fx_snd, fx_rcv, fz_snd, fz_rcv, e_snd, e_rcv, f_snd, f_rcv,
     sa_snd, sa_rcv, sb_snd, sb_rcv, st_snd, st_rcv, x_snd, x_rcv, x2_snd, x2_rcv,
@@ -146,10 +146,15 @@
                 slot = self.wait(1, 1, h)
                 self.put(self.half(slot, h), slot, 12 + h, 3, c, h)
 
-        def finish(self):
+        def near(self):
             for h in range(2):
-                for k, e in ((0, 1), (3, 1), (1, 0), (2, 0), (2, 1)):
+                for k, e in ((0, 1), (3, 1), (1, 0)):
                     self.wait(k, e, h)
+
+        def far(self):
+            for h in range(2):
+                for e in range(2):
+                    self.wait(2, e, h)
 
     smalls = []
     for i, (src, dst) in enumerate((
@@ -266,40 +271,63 @@
 
     lax.fori_loop(0, 8, rows_of, 0)
 
+    def limits(j):
+        consts = tw[j]
+        return consts[:, 0:1] + consts[:, 1:2] + consts[:, 2:3], consts[:, 3:4] + consts[:, 4:5] + consts[:, 5:6]
+
+    for d in range(2):
+        rows = slice(128 * d, 128 * d + 128)
+        for i, column in enumerate(limits(2 * y + d)):
+            lims[i, rows, :] = jnp.broadcast_to(column, (128, 128))
+
     e_all.forward()
 
-    def phi_of(buf, which, out_h, out_l):
-        def block(q, carry):
-            degree_basis(doubled(buf[q]), th, tl)
-            out_h[q] = mm(th[...], pick[which]).astype(BF)
-            out_l[q] = mm(tl[...], pick[which]).astype(BF)
-            return carry
-
-        lax.fori_loop(0, 4, block, 0)
+    def phi_of(buf, which, mine, out_h, out_l):
+        out_h[mine] = mm(th[...], pick[which]).astype(BF)
+        out_l[mine] = mm(tl[...], pick[which]).astype(BF)
+        for k in range(1, 4):
+            q = lax.rem(mine + k, 4)
+            degree_basis(doubled(buf[q]), tph.at[k - 1], tpl.at[k - 1])
+            out_h[q] = mm(tph[k - 1], pick[which]).astype(BF)
+            out_l[q] = mm(tpl[k - 1], pick[which]).astype(BF)
 
     for k in range(1, 4):
         src = lax.rem(x + k, 4)
         remote(fax.at[x], fax.at[src], fx_snd.at[k - 1], fx_rcv.at[src], t, xpeer(k)).wait_recv()
-    phi_of(fax, 0, pha_h, pha_l)
-
-    e_all.finish()
-    for j in range(8):
-        high, low = halves(eh[j])
-        ehl[128 * j:128 * j + 128, 0:128] = high
-        ehl[128 * j:128 * j + 128, 128:256] = low
+    phi_of(fax, 0, x, pha_h, pha_l)
+
+    def split(m):
+        for d in range(2):
+            rows = pl.ds(pl.multiple_of(256 * m + 128 * d, 128), 128)
+            ehl[rows, 0:128], ehl[rows, 128:256] = halves(eh[2 * m + d])
+
+    chip = pl.ds(pl.multiple_of(256 * y, 256), 256)
+
+    def netted(m):
+        cols = pl.ds(pl.multiple_of(256 * m, 256), 256)
+        return mm(same[chip, cols], ehl[cols, :])
+
+    e_all.near()
+    wide = jnp.zeros((256, 256), F32)
+    for k in (0, 1, 3):
+        m = lax.rem(y + k, 4)
+        split(m)
+        wide = wide + netted(m)
+    net = wide[:, :128] + wide[:, 128:] - lims[0]
+    e_all.far()
+    m = lax.rem(y + 2, 4)
+    split(m)
+    wide = netted(m)
+    sas[...] = (lims[1] * jax.nn.sigmoid(net + (wide[:, :128] + wide[:, 128:]))).reshape(2, 128, 128)
 
     def adjoint(j):
         rows = pl.ds(pl.multiple_of(j * 128, 128), 128)
         wide = mm(same[rows, :], ehl[...])
-        consts = tw[j]
-        shift = consts[:, 0:1] + consts[:, 1:2] + consts[:, 2:3]
-        scale = consts[:, 3:4] + consts[:, 4:5] + consts[:, 5:6]
+        shift, scale = limits(j)
         return scale * jax.nn.sigmoid(wide[:, :128] + wide[:, 128:] - shift)
 
     a_all = Gather(sa, sa_snd, sa_rcv, x, lambda k, d: (2 * y + d, xpeer(k)))
     b_all = Gather(sb, sb_snd, sb_rcv, z, lambda k, d: (2 * y + d, zpeer(k)))
-    for d in range(2):
-        sas[d] = adjoint(2 * y + d)
     for e in (1, 0):
         d = lax.rem(c + e, 2)
         a_all.start(sas.at[d, pl.ds(0, 64)], e)
@@ -343,7 +371,7 @@
     for k in range(1, 4):
         src = lax.rem(z + k, 4)
         remote(faz.at[z], faz.at[src], fz_snd.at[k - 1], fz_rcv.at[src], t, zpeer(k)).wait_recv()
-    phi_of(faz, 1, phb_h, phb_l)
+    phi_of(faz, 1, z, phb_h, phb_l)
 
     low_lanes = iota((32, 128), 1) < 64
 
@@ -425,7 +453,7 @@
     grad_b = (grb[0] + grb[1]) + (grb[2] + grb[3])
     grads = jnp.concatenate([grad_a, grad_b], axis=0) * (1.0 / SCEN)
     grads = jnp.concatenate([grads, pltpu.roll(grads, 64, 1)], axis=0).T[0:64, :]
-    coef_out[...] = mm(jnp.concatenate(halves(grads), axis=1), memt[...])
+    grads_out[...] = jnp.concatenate(halves(grads), axis=1)
 
     for k in range(1, 4):
         src = lax.rem(z + k, 4)
@@ -438,10 +466,14 @@
         send.wait_send()
 
 
-def place_outputs(xva, coef, feat, xva_out, coef_out, feat_out, sem):
-    copies = []
-    for i, (src, dst) in enumerate(((coef, coef_out), (feat, feat_out), (xva, xva_out))):
-        copy = pltpu.make_async_copy(src, dst, sem.at[i])
+def place_outputs(xva, feat, grads, memt, xva_out, coef_out, feat_out, coef, sem):
+    copies = [pltpu.make_async_copy(feat, feat_out, sem.at[4]), pltpu.make_async_copy(xva, xva_out, sem.at[5])]
+    for copy in copies:
+        copy.start()
+    for i in range(4):
+        cols = pl.ds(512 * i, 512)
+        coef[i] = mm(grads[...], memt[:, 512 * i:512 * i + 512])
+        copy = pltpu.make_async_copy(coef.at[i], coef_out.at[:, cols], sem.at[i])
         copy.start()
         copies.append(copy)
     for copy in copies:
@@ -458,9 +490,9 @@
         V((1, 128), jnp.int32), V((1, 1024), F32), V((1, 1024), F32),
         V((1024, 2048), F32),
         V((2048, 128), BF),
-        V((256, 2048), BF),
         V((2, 768, 256), BF),
         V((256, 768), BF), V((256, 768), BF),
+        V((3, 256, 768), BF), V((3, 256, 768), BF),
         V((4, 64, 256), F32), V((4, 64, 256), F32),
         V((4, 256, 256), BF), V((4, 256, 256), BF), V((4, 256, 256), BF), V((4, 256, 256), BF),
         V((768, 1024), BF),
@@ -475,6 +507,7 @@
         V((1024, 1024), BF),
         V((256, 1024), BF),
         V((8, 128, 8), F32),
+        V((2, 256, 128), F32),
         V((2, 128, 128), F32),
         V((8, 64, 128), F32), V((8, 64, 128), F32),
         V((2, 8, 128, 128), F32),
@@ -484,16 +517,14 @@
         D((8,)), D((8,)), D((8,)), D((8,)), D(()), D(()), D((7,)), D((8,)), D((3,)), D((4,)),
         D((3,)), D((4,)), D((3,)), D((4,)),
     ]
-    shapes = (
-        jax.ShapeDtypeStruct((1, 128), F32),
-        jax.ShapeDtypeStruct((64, 2048), F32),
-        jax.ShapeDtypeStruct((128, 256), F32),
-    )
+    xva_shape = jax.ShapeDtypeStruct((1, 128), F32)
+    coef_shape = jax.ShapeDtypeStruct((64, 2048), F32)
+    feat_shape = jax.ShapeDtypeStruct((128, 256), F32)
     results = pl.pallas_call(
         kernel,
-        out_shape=shapes,
+        out_shape=(xva_shape, feat_shape, jax.ShapeDtypeStruct((64, 256), BF), jax.ShapeDtypeStruct((256, 2048), BF)),
         in_specs=[hbm] * 8,
-        out_specs=(vmem, vmem, vmem),
+        out_specs=(vmem, vmem, vmem, vmem),
         scratch_shapes=scratch,
         compiler_params=pltpu.CompilerParams(collective_id=0, has_side_effects=True, vmem_limit_bytes=40 << 20),
     )(*[
@@ -505,10 +536,10 @@
     ])
     xva, coef_sens, feature_sens = pl.pallas_call(
         place_outputs,
-        out_shape=shapes,
-        in_specs=[vmem] * 3,
+        out_shape=(xva_shape, coef_shape, feat_shape),
+        in_specs=[vmem] * 4,
         out_specs=(hbm, hbm, hbm),
-        scratch_shapes=[D((3,))],
+        scratch_shapes=[V((4, 64, 512), F32), D((6,))],
         compiler_params=pltpu.CompilerParams(vmem_limit_bytes=4 << 20),
     )(*results)
     return xva.reshape(-1), coef_sens, feature_sens

time: 31 us -> 30.8 us (level)
  no operation moved by 1% of the time
where the time goes in v5:
time: 30.8 us; the launch traced here: 30.7 us
  Pallas kernels  30 us (97%)
  between operations  0.64 us (2%)
    pallas_call x1, Pallas kernels, local(): pl.pallas_call(kernel, out_shape=(xva_shape, feat_shape, jax.ShapeDtypeSt...  29 us
    pallas_call x1, Pallas kernels, local(): pl.pallas_call(place_outputs, out_shape=(xva_shape, coef_shape, feat_shap...  1.04 us

profile of v5, /device:TPU:0, one launch (start us, length us, event | category | flops | bytes accessed | tf_op | source)
XLA Modules:
  0.0 30.7 jit_solution(17788230713505830053)
XLA Ops:
  0.6 29.0 %shard_map.103 = (f32[1,128]{1,0:T(1,128)S(1)}, f32[128,256]{1,0:T(8,128)S(1)}, bf16[64,256]{1,0:T(8,128)(2,1)S(1)}, bf16[256,2048]{1,0:T(8,128)(2,1)S(1)}) custom-call(f32[1024,2048]{1,0:T(8,128)} %coef_hbm.1, f32[64,256]{1,0:T(8,128)} %bitcast.8, s32[1,1024]{1,0:T(1,128)} %bitcast.10, s32[1,1024]{1,0:T(1,128)} %bitcast.11, s32[1,2048]{1,0:T(1,128)} %bitcast.9, ...), custom_call_target="tpu_custom_call" | custom-call | tf_op jit(solution)/shard_map/pallas_call | solution.py:523
  29.6 1.0 %shard_map.104 = (f32[1,128]{1,0:T(1,128)}, f32[64,2048]{1,0:T(8,128)}, f32[128,256]{1,0:T(8,128)}) custom-call(f32[1,128]{1,0:T(1,128)S(1)} %get-tuple-element.10.xva, f32[128,256]{1,0:T(8,128)S(1)} %get-tuple-element.11.feat, bf16[64,256]{1,0:T(8,128)(2,1)S(1)} %get-tuple-element.12.grads, bf16[256,2048]{1,0:T(8,128)(2,1)S(1)} %get-tuple-element.13.memt), custom_call_target="tpu_custom_call" | custom-call | tf_op jit(solution)/shard_map/pallas_call | solution.py:537

commit v6 on v5

--- a/solution.py
+++ b/solution.py
@@ -244,14 +244,6 @@
     eh[t] = etb[c]
     frows[t] = folded[t]
 
-    fvals = jnp.concatenate([ff_ref[...].astype(F32), fd_ref[...].astype(F32), jnp.zeros((6, 1024), F32)], axis=0).astype(BF)
-    lane256 = iota((1024, 256), 1)
-    fidx_a = ((lane256 // 64) * 4 + x) * 64 + lane256 % 64
-    fidx_b = z * 256 + lane256
-    for i, fidx in enumerate((fidx_a, fidx_b)):
-        picked = mm(fvals, onehot(iota((1024, 256), 0) == fidx)).astype(jnp.int32)
-        pick[i] = onehot(iota((768, 256), 0) == (picked[1:2, :] - 1) * 64 + picked[0:1, :])
-
     for k in range(1, 8):
         src = tr(k)
         remote(pos_ref, party.at[src], p_snd.at[k - 1], p_rcv.at[src], src, sigma).wait_recv()
@@ -271,6 +263,16 @@
 
     lax.fori_loop(0, 8, rows_of, 0)
 
+    e_all.forward()
+
+    fvals = jnp.concatenate([ff_ref[...].astype(F32), fd_ref[...].astype(F32), jnp.zeros((6, 1024), F32)], axis=0).astype(BF)
+    lane256 = iota((1024, 256), 1)
+    fidx_a = ((lane256 // 64) * 4 + x) * 64 + lane256 % 64
+    fidx_b = z * 256 + lane256
+    for i, fidx in enumerate((fidx_a, fidx_b)):
+        picked = mm(fvals, onehot(iota((1024, 256), 0) == fidx)).astype(jnp.int32)
+        pick[i] = onehot(iota((768, 256), 0) == (picked[1:2, :] - 1) * 64 + picked[0:1, :])
+
     def limits(j):
         consts = tw[j]
         return consts[:, 0:1] + consts[:, 1:2] + consts[:, 2:3], consts[:, 3:4] + consts[:, 4:5] + consts[:, 5:6]
@@ -279,8 +281,6 @@
         rows = slice(128 * d, 128 * d + 128)
         for i, column in enumerate(limits(2 * y + d)):
             lims[i, rows, :] = jnp.broadcast_to(column, (128, 128))
-
-    e_all.forward()
 
     def phi_of(buf, which, mine, out_h, out_l):
         out_h[mine] = mm(th[...], pick[which]).astype(BF)
@@ -389,11 +389,13 @@
 
     total_a = jnp.zeros((64, 256), F32)
     total_b = jnp.zeros((64, 256), F32)
-    for k in (0, 1, 3, 2):
-        a_all.wait(k)
-        b_all.wait(k)
-        total_a = total_a + gradient(sa, lax.rem(x + k, 4), pha_h, pha_l)
-        total_b = total_b + gradient(sb, lax.rem(z + k, 4), phb_h, phb_l)
+    for near in ((0,), (2,), (1, 3)):
+        for k in near:
+            a_all.wait(k)
+            b_all.wait(k)
+        for k in near:
+            total_a = total_a + gradient(sa, lax.rem(x + k, 4), pha_h, pha_l)
+            total_b = total_b + gradient(sb, lax.rem(z + k, 4), phb_h, phb_l)
     pack(total_a, ga)
     pack(total_b, gb)
     g_sends = []

time: 30.8 us -> 30.6 us (level)
  no operation moved by 1% of the time
where the time goes in v6:
time: 30.6 us; the launch traced here: 30.5 us
  Pallas kernels  29.9 us (98%)
  between operations  0.64 us (2%)
    pallas_call x1, Pallas kernels, local(): pl.pallas_call(kernel, out_shape=(xva_shape, feat_shape, jax.ShapeDtypeSt...  28.8 us
    pallas_call x1, Pallas kernels, local(): pl.pallas_call(place_outputs, out_shape=(xva_shape, coef_shape, feat_shap...  1.04 us

profile of v6, /device:TPU:0, one launch (start us, length us, event | category | flops | bytes accessed | tf_op | source)
XLA Modules:
  0.0 30.5 jit_solution(5178046298383627019)
XLA Ops:
  0.6 28.8 %shard_map.103 = (f32[1,128]{1,0:T(1,128)S(1)}, f32[128,256]{1,0:T(8,128)S(1)}, bf16[64,256]{1,0:T(8,128)(2,1)S(1)}, bf16[256,2048]{1,0:T(8,128)(2,1)S(1)}) custom-call(f32[1024,2048]{1,0:T(8,128)} %coef_hbm.1, f32[64,256]{1,0:T(8,128)} %bitcast.8, s32[1,1024]{1,0:T(1,128)} %bitcast.10, s32[1,1024]{1,0:T(1,128)} %bitcast.11, s32[1,2048]{1,0:T(1,128)} %bitcast.9, ...), custom_call_target="tpu_custom_call" | custom-call | tf_op jit(solution)/shard_map/pallas_call | solution.py:525
  29.5 1.0 %shard_map.104 = (f32[1,128]{1,0:T(1,128)}, f32[64,2048]{1,0:T(8,128)}, f32[128,256]{1,0:T(8,128)}) custom-call(f32[1,128]{1,0:T(1,128)S(1)} %get-tuple-element.10.xva, f32[128,256]{1,0:T(8,128)S(1)} %get-tuple-element.11.feat, bf16[64,256]{1,0:T(8,128)(2,1)S(1)} %get-tuple-element.12.grads, bf16[256,2048]{1,0:T(8,128)(2,1)S(1)} %get-tuple-element.13.memt), custom_call_target="tpu_custom_call" | custom-call | tf_op jit(solution)/shard_map/pallas_call | solution.py:539

commit v7 on v6

--- a/solution.py
+++ b/solution.py
@@ -389,7 +389,27 @@
 
     total_a = jnp.zeros((64, 256), F32)
     total_b = jnp.zeros((64, 256), F32)
+    def second_sums():
+        for k in range(0, 4):
+            for e in range(2):
+                if k == 0 and e == 0:
+                    continue
+                d = lax.rem(c + e, 2)
+                slot = 2 * lax.rem(x + k, 4) + d
+                remote(xr.at[slot], xr.at[slot], x_snd.at[2 * k + e - 1], x_rcv.at[slot], 2 * y + d, xpeer(k)).wait_recv()
+        part = xr[0]
+        for j in range(1, 8):
+            part = part + xr[j]
+        xt[...] = part
+        for k in range(1, 4):
+            send = remote(xt, xz.at[z], x2_snd.at[k - 1], x2_rcv.at[z], t, zpeer(k))
+            send.start()
+            x_sends.append(send)
+        xz[z] = part
+
     for near in ((0,), (2,), (1, 3)):
+        if len(near) > 1:
+            second_sums()
         for k in near:
             a_all.wait(k)
             b_all.wait(k)
@@ -409,22 +429,6 @@
     gra[z] = ga[z]
     grb[x] = gb[x]
 
-    for k in range(0, 4):
-        for e in range(2):
-            if k == 0 and e == 0:
-                continue
-            d = lax.rem(c + e, 2)
-            slot = 2 * lax.rem(x + k, 4) + d
-            remote(xr.at[slot], xr.at[slot], x_snd.at[2 * k + e - 1], x_rcv.at[slot], 2 * y + d, xpeer(k)).wait_recv()
-    part = xr[0]
-    for j in range(1, 8):
-        part = part + xr[j]
-    xt[...] = part
-    for k in range(1, 4):
-        send = remote(xt, xz.at[z], x2_snd.at[k - 1], x2_rcv.at[z], t, zpeer(k))
-        send.start()
-        x_sends.append(send)
-    xz[z] = part
 
     for k in range(1, 8):
         src = tr(k)

time: 30.6 us -> 31.5 us (1.029)
  the two profiles are of different devices: /device:TPU:0 before, /device:TPU:1 now
where the time goes in v7:
time: 31.5 us; the launch traced here: 31.4 us
  Pallas kernels  30.7 us (97%)
  between operations  0.64 us (2%)
    pallas_call x1, Pallas kernels, local(): pl.pallas_call(kernel, out_shape=(xva_shape, feat_shape, jax.ShapeDtypeSt...  29.7 us
    pallas_call x1, Pallas kernels, local(): pl.pallas_call(place_outputs, out_shape=(xva_shape, coef_shape, feat_shap...  1.04 us

profile of v7, /device:TPU:1, one launch (start us, length us, event | category | flops | bytes accessed | tf_op | source)
XLA Modules:
  0.0 31.4 jit_solution(774046566684487486)
XLA Ops:
  0.6 29.7 %shard_map.103 = (f32[1,128]{1,0:T(1,128)S(1)}, f32[128,256]{1,0:T(8,128)S(1)}, bf16[64,256]{1,0:T(8,128)(2,1)S(1)}, bf16[256,2048]{1,0:T(8,128)(2,1)S(1)}) custom-call(f32[1024,2048]{1,0:T(8,128)} %coef_hbm.1, f32[64,256]{1,0:T(8,128)} %bitcast.8, s32[1,1024]{1,0:T(1,128)} %bitcast.10, s32[1,1024]{1,0:T(1,128)} %bitcast.11, s32[1,2048]{1,0:T(1,128)} %bitcast.9, ...), custom_call_target="tpu_custom_call" | custom-call | tf_op jit(solution)/shard_map/pallas_call | solution.py:529
  30.3 1.0 %shard_map.104 = (f32[1,128]{1,0:T(1,128)}, f32[64,2048]{1,0:T(8,128)}, f32[128,256]{1,0:T(8,128)}) custom-call(f32[1,128]{1,0:T(1,128)S(1)} %get-tuple-element.10.xva, f32[128,256]{1,0:T(8,128)S(1)} %get-tuple-element.11.feat, bf16[64,256]{1,0:T(8,128)(2,1)S(1)} %get-tuple-element.12.grads, bf16[256,2048]{1,0:T(8,128)(2,1)S(1)} %get-tuple-element.13.memt), custom_call_target="tpu_custom_call" | custom-call | tf_op jit(solution)/shard_map/pallas_call | solution.py:543
